TPU v7x, 32 devices: a whole 2x2x4 slice. The times are simulated.
32 devices in a mesh: dp: 4 (over x, core), ctx: 4 (over z), mp: 2 (over y).
Axes of the slice: x: 2, y: 2, z: 4, core: 2. Of those that a mesh axis runs over, the one named last changes fastest.
Arguments:
- block_input: bfloat16 [8, 512, 2048], P('dp', 'ctx'), may hold values from -6 to 6
- doc_positions: int32 [8, 512], P('dp', 'ctx'), may hold values from 0 to 383, as said below
- out_cotangent: bfloat16 [8, 512, 2048], P('dp', 'ctx'), may hold values from -6 to 6
- attn_gain: bfloat16 [2048], P(('dp', 'ctx')), may hold values from 0.099609375 to 1.8984375
- mlp_gain: bfloat16 [2048], P(('dp', 'ctx')), may hold values from 0.099609375 to 1.8984375
- query_gain: bfloat16 [128], P(('dp', 'ctx')), may hold values from 0.099609375 to 1.8984375
- key_gain: bfloat16 [128], P(('dp', 'ctx')), may hold values from 0.099609375 to 1.8984375
- w_query: bfloat16 [2048, 2048], P(('dp', 'ctx'), 'mp'), may hold values from -0.125 to 0.125
- w_key: bfloat16 [2048, 1024], P(('dp', 'ctx'), 'mp'), may hold values from -0.125 to 0.125
- w_value: bfloat16 [2048, 1024], P(('dp', 'ctx'), 'mp'), may hold values from -0.125 to 0.125
- w_out: bfloat16 [2048, 2048], P('mp', ('dp', 'ctx')), may hold values from -2 to 2
- w_gate: bfloat16 [2048, 6144], P(('dp', 'ctx'), 'mp'), may hold values from -0.125 to 0.125
- w_up: bfloat16 [2048, 6144], P(('dp', 'ctx'), 'mp'), may hold values from -0.125 to 0.125
- w_down: bfloat16 [6144, 2048], P('mp', ('dp', 'ctx')), may hold values from -0.078125 to 0.078125
Outputs:
- block_output: bfloat16 [8, 512, 2048], P('dp', 'ctx')
- input_grad: float32 [8, 512, 2048], P('dp', 'ctx')
- attn_gain_grad: float32 [2048], P(('dp', 'ctx'))
- mlp_gain_grad: float32 [2048], P(('dp', 'ctx'))
- query_gain_grad: float32 [128], P(('dp', 'ctx'))
- key_gain_grad: float32 [128], P(('dp', 'ctx'))
- w_query_grad: float32 [2048, 2048], P(('dp', 'ctx'), 'mp')
- w_key_grad: float32 [2048, 1024], P(('dp', 'ctx'), 'mp')
- w_value_grad: float32 [2048, 1024], P(('dp', 'ctx'), 'mp')
- w_out_grad: float32 [2048, 2048], P('mp', ('dp', 'ctx'))
- w_gate_grad: float32 [2048, 6144], P(('dp', 'ctx'), 'mp')
- w_up_grad: float32 [2048, 6144], P(('dp', 'ctx'), 'mp')
- w_down_grad: float32 [6144, 2048], P('mp', ('dp', 'ctx'))
Inputs may be any that keep to these rules, and one draw needn't show every extreme that they name: `doc_positions`: each sequence holds two documents: positions count up from 0 at its start and again from 0 at a boundary between 128 and 384; the first sequence's boundary is at 128.
All inputs are finite; a program needn't handle non-finite values.
Results may differ from a plain program's by a relative error of at most 0.019.
Values may be sent and summed in bfloat16 or wider, within the bound.
A program may use at most 256 MiB of HBM per device.

v0:
```python
import jax
import jax.numpy as jnp
from jax import lax
from jax.sharding import PartitionSpec as P

eps_norm = 1e-06
rope_base = 1000000.0


def rms_scale(value_rows):
    return lax.rsqrt(jnp.mean(value_rows * value_rows, axis=-1, keepdims=True) + eps_norm)


def rope_tables(places, head_size):
    half_size = head_size // 2
    inverse = rope_base ** (-2.0 * jnp.arange(half_size).astype(jnp.float32) / head_size)
    angles = places.astype(jnp.float32)[:, None] * inverse[None, :]
    angles = jnp.concatenate([angles, angles], axis=-1)
    return (jnp.cos(angles), jnp.sin(angles))


def rotate(values, cosine, sine):
    half_size = values.shape[-1] // 2
    turned = jnp.concatenate([-values[..., half_size:], values[..., :half_size]], axis=-1)
    return values * cosine[:, None, :] + turned * sine[:, None, :]


def rotate_back(grads, cosine, sine):
    half_size = grads.shape[-1] // 2
    weighted = grads * sine[:, None, :]
    return grads * cosine[:, None, :] + jnp.concatenate(
        [weighted[..., half_size:], -weighted[..., :half_size]], axis=-1
    )


def block_mask(query_index, lowest, key_index):
    return (key_index[None, :] <= query_index[:, None]) & (key_index[None, :] >= lowest[:, None])


def dot_nt(left, right):
    return lax.dot_general(
        left, right, (((1,), (1,)), ((), ())), preferred_element_type=jnp.float32
    )


def dot_tn(left, right):
    return lax.dot_general(
        left, right, (((0,), (0,)), ((), ())), preferred_element_type=jnp.float32
    )


def micro_pass(inputs_seq, places, cotangent, shards, totals):
    float_type = jnp.float32
    half_type = jnp.bfloat16
    fetched = (
        lax.all_gather(shards[0], ("dp", "ctx"), axis=0, tiled=True),
        lax.all_gather(shards[1], ("dp", "ctx"), axis=0, tiled=True),
        lax.all_gather(shards[2], ("dp", "ctx"), axis=0, tiled=True),
        lax.all_gather(shards[3], ("dp", "ctx"), axis=0, tiled=True),
        lax.all_gather(shards[4], ("dp", "ctx"), axis=0, tiled=True),
        lax.all_gather(shards[5], ("dp", "ctx"), axis=0, tiled=True),
        lax.all_gather(shards[6], ("dp", "ctx"), axis=0, tiled=True),
        lax.all_gather(shards[7], ("dp", "ctx"), axis=1, tiled=True),
        lax.all_gather(shards[8], ("dp", "ctx"), axis=0, tiled=True),
        lax.all_gather(shards[9], ("dp", "ctx"), axis=0, tiled=True),
        lax.all_gather(shards[10], ("dp", "ctx"), axis=1, tiled=True),
    )
    gain_attn = fetched[0].astype(float_type)
    gain_mlp = fetched[1].astype(float_type)
    gain_query = fetched[2].astype(float_type)
    gain_key = fetched[3].astype(float_type)
    query_proj, key_proj, value_proj, out_proj, gate_proj, up_proj, down_proj = fetched[4:]
    head_size = gain_query.shape[0]
    head_count = query_proj.shape[1] // head_size
    kv_count = key_proj.shape[1] // head_size
    group_size = head_count // kv_count
    token_count = inputs_seq.shape[0]
    ctx_count = lax.axis_size("ctx")
    ctx_rank = lax.axis_index("ctx")
    scaling = head_size ** (-0.5)
    query_index = ctx_rank * token_count + jnp.arange(token_count, dtype=jnp.int32)
    lowest = query_index - places
    last_query = ctx_rank * token_count + token_count - 1
    residual_in = inputs_seq.astype(float_type)
    scale_attn = rms_scale(residual_in)
    normed_attn = residual_in * scale_attn
    attn_input = (normed_attn * gain_attn).astype(half_type)
    query_raw = jnp.dot(attn_input, query_proj, preferred_element_type=float_type).reshape(
        token_count, head_count, head_size
    )
    key_raw = jnp.dot(attn_input, key_proj, preferred_element_type=float_type).reshape(
        token_count, kv_count, head_size
    )
    value_rows = jnp.dot(attn_input, value_proj, preferred_element_type=float_type).astype(
        half_type
    )
    query_scale = rms_scale(query_raw)
    query_normed = query_raw * query_scale
    key_scale = rms_scale(key_raw)
    key_normed = key_raw * key_scale
    cosine, sine = rope_tables(places, head_size)
    query_rot = rotate(query_normed * gain_query, cosine, sine).astype(half_type)
    key_rot = (
        rotate(key_normed * gain_key, cosine, sine)
        .astype(half_type)
        .reshape(token_count, kv_count * head_size)
    )
    query_group = query_rot.reshape(token_count, kv_count, group_size, head_size)
    initial = (
        jnp.full((kv_count, group_size, token_count), -1e30, float_type),
        jnp.zeros((kv_count, group_size, token_count), float_type),
        jnp.zeros((token_count, kv_count, group_size, head_size), float_type),
    )
    pieces = (
        lax.all_gather(key_rot, "ctx", axis=0, tiled=True),
        lax.all_gather(value_rows, "ctx", axis=0, tiled=True),
    )
    row_count = pieces[0].shape[0]
    key_piece = pieces[0].reshape(row_count, kv_count, head_size)
    value_piece = pieces[1].reshape(row_count, kv_count, head_size)

    def fold_attend(state):
        peak, total, running = state
        scores = (
            jnp.einsum("qkgd,jkd->kgqj", query_group, key_piece, preferred_element_type=float_type)
            * scaling
        )
        allowed = block_mask(query_index, lowest, jnp.arange(row_count, dtype=jnp.int32))
        new_peak = jnp.maximum(peak, jnp.max(jnp.where(allowed, scores, -jnp.inf), axis=-1))
        weights = jnp.where(allowed, jnp.exp(scores - new_peak[..., None]), 0.0)
        total = jnp.sum(weights, axis=-1)
        running = jnp.einsum(
            "kgqj,jkd->qkgd",
            weights.astype(half_type),
            value_piece,
            preferred_element_type=float_type,
        )
        return (new_peak, total, running)

    peak, total, running = lax.cond(
        jnp.int32(0) <= last_query, fold_attend, lambda state: state, initial
    )
    attn_rows = (
        (running / jnp.transpose(total, (2, 0, 1))[..., None])
        .astype(half_type)
        .reshape(token_count, head_count * head_size)
    )
    log_total = peak + jnp.log(total)
    attn_out = lax.psum(
        jnp.dot(attn_rows, out_proj, preferred_element_type=float_type).astype(jnp.bfloat16), "mp"
    ).astype(jnp.float32)
    middle = residual_in + attn_out
    scale_mlp = rms_scale(middle)
    normed_mlp = middle * scale_mlp
    mlp_input = (normed_mlp * gain_mlp).astype(half_type)
    gate_rows = jnp.dot(mlp_input, gate_proj, preferred_element_type=float_type)
    up_rows = jnp.dot(mlp_input, up_proj, preferred_element_type=float_type)
    sigmoid_gate = jax.nn.sigmoid(gate_rows)
    hidden_rows = (gate_rows * sigmoid_gate * up_rows).astype(half_type)
    mlp_out = lax.psum(
        jnp.dot(hidden_rows, down_proj, preferred_element_type=float_type).astype(jnp.bfloat16),
        "mp",
    ).astype(jnp.float32)
    block_output = (middle + mlp_out).astype(half_type)
    refetched = (
        lax.all_gather(shards[0], ("dp", "ctx"), axis=0, tiled=True),
        lax.all_gather(shards[1], ("dp", "ctx"), axis=0, tiled=True),
        lax.all_gather(shards[2], ("dp", "ctx"), axis=0, tiled=True),
        lax.all_gather(shards[3], ("dp", "ctx"), axis=0, tiled=True),
        lax.all_gather(shards[4], ("dp", "ctx"), axis=0, tiled=True),
        lax.all_gather(shards[5], ("dp", "ctx"), axis=0, tiled=True),
        lax.all_gather(shards[6], ("dp", "ctx"), axis=0, tiled=True),
        lax.all_gather(shards[7], ("dp", "ctx"), axis=1, tiled=True),
        lax.all_gather(shards[8], ("dp", "ctx"), axis=0, tiled=True),
        lax.all_gather(shards[9], ("dp", "ctx"), axis=0, tiled=True),
        lax.all_gather(shards[10], ("dp", "ctx"), axis=1, tiled=True),
    )
    gain_attn = refetched[0].astype(float_type)
    gain_mlp = refetched[1].astype(float_type)
    gain_query = refetched[2].astype(float_type)
    gain_key = refetched[3].astype(float_type)
    query_proj, key_proj, value_proj, out_proj, gate_proj, up_proj, down_proj = refetched[4:]
    down_grad = dot_tn(hidden_rows, cotangent)
    hidden_grad = dot_nt(cotangent, down_proj)
    gate_grad = (
        hidden_grad * up_rows * sigmoid_gate * (1.0 + gate_rows * (1.0 - sigmoid_gate))
    ).astype(half_type)
    up_grad = (hidden_grad * gate_rows * sigmoid_gate).astype(half_type)
    gate_proj_grad = dot_tn(mlp_input, gate_grad)
    up_proj_grad = dot_tn(mlp_input, up_grad)
    mlp_in_grad = lax.psum(
        (dot_nt(gate_grad, gate_proj) + dot_nt(up_grad, up_proj)).astype(jnp.bfloat16), "mp"
    ).astype(jnp.float32)
    mlp_gain_grad = jnp.sum(mlp_in_grad * normed_mlp, axis=0)
    normed_grad = mlp_in_grad * gain_mlp
    middle_grad = cotangent.astype(float_type) + scale_mlp * (
        normed_grad - normed_mlp * jnp.mean(normed_grad * normed_mlp, axis=-1, keepdims=True)
    )
    middle_half = middle_grad.astype(half_type)
    out_proj_grad = dot_tn(attn_rows, middle_half)
    attn_grad = dot_nt(middle_half, out_proj).astype(half_type)
    grad_group = attn_grad.reshape(token_count, kv_count, group_size, head_size)
    attn_group = attn_rows.reshape(token_count, kv_count, group_size, head_size)
    row_dot = jnp.einsum(
        "qkgd,qkgd->kgq", grad_group, attn_group, preferred_element_type=float_type
    )
    key_back, value_back = (
        lax.all_gather(key_rot, "ctx", axis=0, tiled=True),
        lax.all_gather(value_rows, "ctx", axis=0, tiled=True),
    )

    def back_block(query_sum, block_id):
        start = block_id * token_count
        key_piece = lax.dynamic_slice_in_dim(key_back, start, token_count, 0).reshape(
            token_count, kv_count, head_size
        )
        value_piece = lax.dynamic_slice_in_dim(value_back, start, token_count, 0).reshape(
            token_count, kv_count, head_size
        )

        def back_attend(running):
            scores = (
                jnp.einsum(
                    "qkgd,jkd->kgqj", query_group, key_piece, preferred_element_type=float_type
                )
                * scaling
            )
            allowed = block_mask(
                query_index, lowest, start + jnp.arange(token_count, dtype=jnp.int32)
            )
            probs = jnp.where(allowed, jnp.exp(scores - log_total[..., None]), 0.0)
            value_part = jnp.einsum(
                "kgqj,qkgd->jkd",
                probs.astype(half_type),
                grad_group,
                preferred_element_type=float_type,
            )
            prob_grad = jnp.einsum(
                "qkgd,jkd->kgqj", grad_group, value_piece, preferred_element_type=float_type
            )
            score_half = (probs * (prob_grad - row_dot[..., None])).astype(half_type)
            query_part = (
                jnp.einsum(
                    "kgqj,jkd->qkgd", score_half, key_piece, preferred_element_type=float_type
                )
                * scaling
            )
            key_part = (
                jnp.einsum(
                    "kgqj,qkgd->jkd", score_half, query_group, preferred_element_type=float_type
                )
                * scaling
            )
            return (
                running + query_part,
                jnp.concatenate(
                    [
                        key_part.reshape(token_count, kv_count * head_size),
                        value_part.reshape(token_count, kv_count * head_size),
                    ],
                    axis=-1,
                ),
            )

        def passing(running):
            return (running, jnp.zeros((token_count, 2 * kv_count * head_size), float_type))

        return lax.cond(start <= last_query, back_attend, passing, query_sum)

    query_grad, kv_terms = lax.scan(
        back_block,
        jnp.zeros((token_count, kv_count, group_size, head_size), float_type),
        jnp.arange(ctx_count, dtype=jnp.int32),
    )
    kv_grad = lax.psum_scatter(
        kv_terms.reshape(ctx_count * token_count, 2 * kv_count * head_size).astype(jnp.bfloat16),
        "ctx",
        scatter_dimension=0,
        tiled=True,
    ).astype(jnp.float32)
    key_rot_grad = kv_grad[:, : kv_count * head_size].reshape(token_count, kv_count, head_size)
    value_half = kv_grad[:, kv_count * head_size :].astype(half_type)
    query_back = rotate_back(query_grad.reshape(token_count, head_count, head_size), cosine, sine)
    key_grad_back = rotate_back(key_rot_grad, cosine, sine)
    query_gain_part = jnp.sum(query_back * query_normed, axis=(0, 1))
    key_gain_part = jnp.sum(key_grad_back * key_normed, axis=(0, 1))
    query_ngrad = query_back * gain_query
    key_ngrad = key_grad_back * gain_key
    query_half = (
        (
            query_scale
            * (
                query_ngrad
                - query_normed * jnp.mean(query_ngrad * query_normed, axis=-1, keepdims=True)
            )
        )
        .reshape(token_count, head_count * head_size)
        .astype(half_type)
    )
    key_half = (
        (
            key_scale
            * (key_ngrad - key_normed * jnp.mean(key_ngrad * key_normed, axis=-1, keepdims=True))
        )
        .reshape(token_count, kv_count * head_size)
        .astype(half_type)
    )
    query_proj_grad = dot_tn(attn_input, query_half)
    key_proj_grad = dot_tn(attn_input, key_half)
    value_proj_grad = dot_tn(attn_input, value_half)
    attn_in_grad, query_gain_sum, key_gain_sum = (
        lax.psum(
            (
                dot_nt(query_half, query_proj)
                + dot_nt(key_half, key_proj)
                + dot_nt(value_half, value_proj)
            ).astype(jnp.bfloat16),
            "mp",
        ).astype(jnp.float32),
        lax.psum(query_gain_part.astype(jnp.bfloat16), "mp").astype(jnp.float32),
        lax.psum(key_gain_part.astype(jnp.bfloat16), "mp").astype(jnp.float32),
    )
    attn_gain_grad = jnp.sum(attn_in_grad * normed_attn, axis=0)
    normed_in_grad = attn_in_grad * gain_attn
    input_grad = middle_grad + scale_attn * (
        normed_in_grad
        - normed_attn * jnp.mean(normed_in_grad * normed_attn, axis=-1, keepdims=True)
    )
    addition = (
        attn_gain_grad,
        mlp_gain_grad,
        query_gain_sum,
        key_gain_sum,
        query_proj_grad,
        key_proj_grad,
        value_proj_grad,
        out_proj_grad,
        gate_proj_grad,
        up_proj_grad,
        down_grad,
    )
    totals = tuple((earlier + later for earlier, later in zip(totals, addition)))
    return (block_output, input_grad, totals)


def on_device(
    block_input,
    doc_positions,
    out_cotangent,
    attn_gain,
    mlp_gain,
    query_gain,
    key_gain,
    w_query,
    w_key,
    w_value,
    w_out,
    w_gate,
    w_up,
    w_down,
):
    shards = (
        attn_gain,
        mlp_gain,
        query_gain,
        key_gain,
        w_query,
        w_key,
        w_value,
        w_out,
        w_gate,
        w_up,
        w_down,
    )
    head_size = query_gain.shape[0] * lax.axis_size(("dp", "ctx"))
    model_width = block_input.shape[2]
    query_width = w_query.shape[1]
    kv_width = w_key.shape[1]
    hidden_width = w_gate.shape[1]
    totals = (
        jnp.zeros((model_width,), jnp.float32),
        jnp.zeros((model_width,), jnp.float32),
        jnp.zeros((head_size,), jnp.float32),
        jnp.zeros((head_size,), jnp.float32),
        jnp.zeros((model_width, query_width), jnp.float32),
        jnp.zeros((model_width, kv_width), jnp.float32),
        jnp.zeros((model_width, kv_width), jnp.float32),
        jnp.zeros((query_width, model_width), jnp.float32),
        jnp.zeros((model_width, hidden_width), jnp.float32),
        jnp.zeros((model_width, hidden_width), jnp.float32),
        jnp.zeros((hidden_width, model_width), jnp.float32),
    )
    output_list = []
    grad_list = []
    for micro in range(block_input.shape[0]):
        output_rows, input_rows, totals = micro_pass(
            block_input[micro], doc_positions[micro], out_cotangent[micro], shards, totals
        )
        output_list.append(output_rows)
        grad_list.append(input_rows)
    owned = (
        lax.psum_scatter(totals[0], ("dp", "ctx"), scatter_dimension=0, tiled=True),
        lax.psum_scatter(totals[1], ("dp", "ctx"), scatter_dimension=0, tiled=True),
        lax.psum_scatter(totals[2], ("dp", "ctx"), scatter_dimension=0, tiled=True),
        lax.psum_scatter(totals[3], ("dp", "ctx"), scatter_dimension=0, tiled=True),
        lax.psum_scatter(totals[4], ("dp", "ctx"), scatter_dimension=0, tiled=True),
        lax.psum_scatter(totals[5], ("dp", "ctx"), scatter_dimension=0, tiled=True),
        lax.psum_scatter(totals[6], ("dp", "ctx"), scatter_dimension=0, tiled=True),
        lax.psum_scatter(totals[7], ("dp", "ctx"), scatter_dimension=1, tiled=True),
        lax.psum_scatter(totals[8], ("dp", "ctx"), scatter_dimension=0, tiled=True),
        lax.psum_scatter(totals[9], ("dp", "ctx"), scatter_dimension=0, tiled=True),
        lax.psum_scatter(totals[10], ("dp", "ctx"), scatter_dimension=1, tiled=True),
    )
    return (
        jnp.stack(output_list),
        jnp.stack(grad_list),
        owned[0],
        owned[1],
        owned[2],
        owned[3],
        owned[4],
        owned[5],
        owned[6],
        owned[7],
        owned[8],
        owned[9],
        owned[10],
    )


def solution(mesh):
    in_specs = (
        P("dp", "ctx", None),
        P("dp", "ctx"),
        P("dp", "ctx", None),
        P(("dp", "ctx")),
        P(("dp", "ctx")),
        P(("dp", "ctx")),
        P(("dp", "ctx")),
        P(("dp", "ctx"), "mp"),
        P(("dp", "ctx"), "mp"),
        P(("dp", "ctx"), "mp"),
        P("mp", ("dp", "ctx")),
        P(("dp", "ctx"), "mp"),
        P(("dp", "ctx"), "mp"),
        P("mp", ("dp", "ctx")),
    )
    out_specs = (
        P("dp", "ctx", None),
        P("dp", "ctx", None),
        P(("dp", "ctx")),
        P(("dp", "ctx")),
        P(("dp", "ctx")),
        P(("dp", "ctx")),
        P(("dp", "ctx"), "mp"),
        P(("dp", "ctx"), "mp"),
        P(("dp", "ctx"), "mp"),
        P("mp", ("dp", "ctx")),
        P(("dp", "ctx"), "mp"),
        P(("dp", "ctx"), "mp"),
        P("mp", ("dp", "ctx")),
    )
    return jax.shard_map(
        on_device, mesh=mesh, in_specs=in_specs, out_specs=out_specs, check_vma=False
    )
```

profile of v0, /device:TPU:0, one launch (start us, length us, event | category | flops | bytes accessed | tf_op | source)
XLA Modules:
  0.0 1952.1 jit_solution(1169991209637501407)
XLA Ops:
  10.0 34.1 %all-gather = bf16[16,1,128]{2,1,0:T(2,128)(2,1)S(1)} all-gather(bf16[1,1,128]{2,1,0:T(2,128)(2,1)} %bitcast.483), channel_id=1, replica_groups=mesh['dp'=4,'ctx'=4,'mp'=2] {'dp','ctx'}, dimensions={0}, use_global_device_ids=true | all-gather | bytes 4352 | tf_op jit(solution)/shard_map/all_gather | solution.py:56
  47.9 29.9 %all-reduce.7 = (bf16[128]{0:T(256)(128)(2,1)S(1)}, bf16[128]{0:T(256)(128)(2,1)S(1)}) all-reduce(bf16[128]{0:T(256)(128)(2,1)S(1)} %dynamic-update-slice, bf16[128]{0:T(256)(128)(2,1)S(1)} %dynamic-update-slice.1), channel_id=1, replica_groups=mesh['dp'=4,'ctx'=4,'mp'=2] {'dp','ctx'}, use_global_device_ids=true, to_apply=%add | all-reduce | flops 256 | bytes 1024
  80.9 4.0 copy.115
  89.0 15.8 all_gather.43
  107.2 20.1 %all_gather.44 = bf16[512,512]{1,0:T(8,128)(2,1)} all-gather(bf16[128,512]{1,0:T(8,128)(2,1)S(1)} %convolution_convert_fusion.6), channel_id=1, replica_groups=mesh['dp'=4,'ctx'=4,'mp'=2] {'ctx'}, dimensions={0}, use_global_device_ids=true | all-gather | bytes 655360 | tf_op jit(solution)/shard_map/all_gather | solution.py:116
  127.4 24.0 %all_gather.33 = bf16[512,512]{0,1:T(8,128)(2,1)S(1)} all-gather(bf16[128,512]{0,1:T(8,128)(2,1)S(1)} %bitcast.479), channel_id=1, replica_groups=mesh['dp'=4,'ctx'=4,'mp'=2] {'ctx'}, dimensions={0}, use_global_device_ids=true | all-gather | bytes 655360 | tf_op jit(solution)/shard_map/all_gather | solution.py:115
  151.9 19.9 %all_gather.37 = bf16[512,512]{1,0:T(8,128)(2,1)} all-gather(bf16[128,512]{1,0:T(8,128)(2,1)S(1)} %convolution_convert_fusion.7), channel_id=1, replica_groups=mesh['dp'=4,'ctx'=4,'mp'=2] {'ctx'}, dimensions={0}, use_global_device_ids=true | all-gather | bytes 655360 | tf_op jit(solution)/shard_map/all_gather | solution.py:116
  171.8 6.5 copy.116
  184.4 9.8 conditional.5
  195.5 8.7 conditional.4
  206.6 6.7 all-gather.16.cloned.1.call-done
  213.3 3.9 convolution_convert_fusion.1
  220.9 30.2 %all-gather.1 = bf16[16,1,128]{2,1,0:T(2,128)(2,1)S(1)} all-gather(bf16[1,1,128]{2,1,0:T(2,128)(2,1)S(1)} %bitcast.484), channel_id=1, replica_groups=mesh['dp'=4,'ctx'=4,'mp'=2] {'dp','ctx'}, dimensions={0}, use_global_device_ids=true | all-gather | bytes 4352 | tf_op jit(solution)/shard_map/all_gather | solution.py:57
  259.5 100.3 %all-gather.18.cloned.1.call-done = bf16[2048,3072]{1,0:T(8,128)(2,1)} async-done(((bf16[128,3072]{1,0:T(8,128)(2,1)}), bf16[2048,3072]{1,0:T(8,128)(2,1)}) %all-gather.18.cloned.1.call-update) | async-done | bytes 12582928 | tf_op jit(solution)/shard_map/all_gather | solution.py:64
  359.8 7.5 fusion.180
  367.3 93.5 %all-gather.20.cloned.1.call-done = bf16[2048,3072]{1,0:T(8,128)(2,1)} async-done(((bf16[128,3072]{1,0:T(8,128)(2,1)}), bf16[2048,3072]{1,0:T(8,128)(2,1)}) %all-gather.20.cloned.1.call-update) | async-done | bytes 12582928 | tf_op jit(solution)/shard_map/all_gather | solution.py:65
  460.8 7.7 fusion.181
  477.5 87.3 %all-gather.22.cloned.1.call-done = bf16[3072,2048]{1,0:T(8,128)(2,1)} async-done(((bf16[3072,128]{1,0:T(8,128)(2,1)}), bf16[3072,2048]{1,0:T(8,128)(2,1)}) %all-gather.22.cloned.1.call-update) | async-done | bytes 12582928 | tf_op jit(solution)/shard_map/all_gather | solution.py:66
  564.8 11.3 multiply_convert_fusion
  576.2 10.1 fusion.184
  586.3 11.7 multiply_convert_fusion.2
  598.0 10.2 fusion.182
  608.2 6.9 fusion.57
  615.1 6.5 fusion.56
  621.7 7.8 convolution_convert_fusion
  629.6 7.3 convolution_convert_fusion.2
  636.9 23.2 %all-reduce.18.cloned.1.call-done = (bf16[128,2048]{1,0:T(8,128)(2,1)}, bf16[128,2048]{1,0:T(8,128)(2,1)}) async-done(((bf16[128,2048]{1,0:T(8,128)(2,1)}, bf16[128,2048]{1,0:T(8,128)(2,1)}), (bf16[128,2048]{1,0:T(8,128)(2,1)}, bf16[128,2048]{1,0:T(8,128)(2,1)})) %all-reduce.18.cloned.1.call-update) | async-done | bytes 1048592 | tf_op jit(solution)/shard_map/psum | solution.py:191
  668.8 4.0 convolution_convert_fusion.5
  679.4 11.8 while.33
  697.0 11.5 while.32
  718.5 12.5 reduce-scatter.12.cloned.1.call-done
  734.4 25.3 %reduce-scatter.10.cloned.1.call-done = bf16[128,1024]{1,0:T(8,128)(2,1)} async-done(((bf16[512,1024]{1,0:T(8,128)(2,1)}), bf16[128,1024]{1,0:T(8,128)(2,1)}) %reduce-scatter.10.cloned.1.call-update) | async-done | bytes 262160 | tf_op jit(solution)/shard_map/reduce_scatter | solution.py:275
  783.4 4.7 convolution_add_fusion.4
  790.8 4.6 convolution_add_fusion.3
  796.5 11.4 fusion.186
  807.8 17.9 convolution_add_fusion.1
  825.8 11.3 fusion.187
  837.1 16.8 convolution_add_fusion
  855.1 11.4 fusion.117
  866.5 16.9 convolution_add_fusion.2
  885.0 4.9 all-reduce.8
  892.0 60.7 %all-reduce.6 = (f32[2048]{0:T(1024)S(1)}, f32[2048]{0:T(1024)S(1)}, f32[128]{0:T(128)S(1)}, f32[128]{0:T(128)S(1)}) all-reduce(f32[2048]{0:T(1024)S(1)} %add.338, f32[2048]{0:T(1024)S(1)} %add.339, f32[128]{0:T(128)S(1)} %convert_add_fusion.1, f32[128]{0:T(128)S(1)} %convert_add_fusion), channel_id=4, replica_groups=mesh['dp'=4,'ctx'=4,'mp'=2] {'dp','ctx'}, use_global_device_ids=true, to_apply=%region_44.45.clone | all-reduce | flops 4352 | bytes 34816
  960.6 28.1 %reduce-scatter.18.cloned.1.call-done = f32[128,512]{1,0:T(8,128)} async-done(((f32[2048,512]{1,0:T(8,128)}), f32[128,512]{1,0:T(8,128)}) %reduce-scatter.18.cloned.1.call-update) | async-done | bytes 262160 | tf_op jit(solution)/shard_map/reduce_scatter | solution.py:408
  988.7 107.0 %reduce-scatter.14.cloned.1.call-done = f32[128,1024]{1,0:T(8,128)} async-done(((f32[2048,1024]{1,0:T(8,128)}), f32[128,1024]{1,0:T(8,128)}) %reduce-scatter.14.cloned.1.call-update) | async-done | bytes 524304 | tf_op jit(solution)/shard_map/reduce_scatter | solution.py:406
  1095.7 107.7 %reduce-scatter.20.cloned.1.call-done = f32[1024,128]{1,0:T(8,128)} async-done(((f32[1024,2048]{1,0:T(8,128)}), f32[1024,128]{1,0:T(8,128)}) %reduce-scatter.20.cloned.1.call-update) | async-done | bytes 524304 | tf_op jit(solution)/shard_map/reduce_scatter | solution.py:409
  1203.5 247.7 %reduce-scatter.22.cloned.1.call-done = f32[128,3072]{1,0:T(8,128)} async-done(((f32[2048,3072]{1,0:T(8,128)}), f32[128,3072]{1,0:T(8,128)}) %reduce-scatter.22.cloned.1.call-update) | async-done | bytes 1572880 | tf_op jit(solution)/shard_map/reduce_scatter | solution.py:410
  1451.2 247.2 %reduce-scatter.24.cloned.1.call-done = f32[128,3072]{1,0:T(8,128)} async-done(((f32[2048,3072]{1,0:T(8,128)}), f32[128,3072]{1,0:T(8,128)}) %reduce-scatter.24.cloned.1.call-update) | async-done | bytes 1572880 | tf_op jit(solution)/shard_map/reduce_scatter | solution.py:411
  1698.3 247.0 %reduce-scatter.26.cloned.1.call-done = f32[3072,128]{1,0:T(8,128)} async-done(((f32[3072,2048]{1,0:T(8,128)}), f32[3072,128]{1,0:T(8,128)}) %reduce-scatter.26.cloned.1.call-update) | async-done | bytes 1572880 | tf_op jit(solution)/shard_map/reduce_scatter | solution.py:412
  (426 shorter events, 161.3 us)
Async XLA Ops:
  7.2 73.7 %copy-start.78 = (s32[2,128]{1,0:T(2,128)S(1)}, s32[2,128]{1,0:T(2,128)}, u32[]{:S(2)}) copy-start(s32[2,128]{1,0:T(2,128)} %param.27) | copy-start | bytes 3076
  7.2 73.7 %all-gather.10.cloned.1.call-start = ((), (), s32[]{:S(2)}) async-start(), calls=%async_computation.9 | async-start | bytes 2228224 | tf_op jit(solution)/shard_map/all_gather | solution.py:61
  7.9 96.9 %all-gather.14.cloned.1.call-start = ((), (), s32[]{:S(2)}) async-start(), calls=%async_computation.11 | async-start | bytes 2228224 | tf_op jit(solution)/shard_map/all_gather | solution.py:62
  8.7 163.1 %all-gather.12.cloned.1.call-start = ((), (), s32[]{:S(2)}) async-start(), calls=%async_computation.10 | async-start | bytes 4456448 | tf_op jit(solution)/shard_map/all_gather | solution.py:60
  9.4 203.9 %all-gather.16.cloned.1.call-start = ((), (), s32[]{:S(2)}) async-start(), calls=%async_computation.12 | async-start | bytes 4456448 | tf_op jit(solution)/shard_map/all_gather | solution.py:63
  10.0 247.2 %all-reduce.20.cloned.1.call-start = ((), (), s32[]{:S(2)}) async-start(), calls=%async_computation.27 | async-start | bytes 2097152 | tf_op jit(solution)/shard_map/psum | solution.py:149
  77.8 105.5 %copy-start.72 = (f32[128]{0:T(128)}, f32[128]{0:T(128)S(1)}, u32[]{:S(2)}) copy-start(f32[128]{0:T(128)S(1)} %convert_element_type.333) | copy-start | bytes 1540
  79.2 104.9 %copy-start.59 = (f32[128,128]{0,1:T(8,128)}, f32[128,128]{0,1:T(8,128)S(1)}, u32[]{:S(2)}) copy-start(f32[128,128]{0,1:T(8,128)S(1)} %get-tuple-element.799) | copy-start | bytes 196612
  80.9 101.1 %copy-start.68 = (f32[128]{0:T(128)}, f32[128]{0:T(128)S(1)}, u32[]{:S(2)}) copy-start(f32[128]{0:T(128)S(1)} %add_rsqrt_fusion.5) | copy-start | bytes 1540
  80.9 103.3 %copy-start.66 = (s32[128]{0:T(128)}, s32[128]{0:T(128)S(1)}, u32[]{:S(2)}) copy-start(s32[128]{0:T(128)S(1)} %get-tuple-element.998) | copy-start | bytes 1540
  104.8 79.4 %copy-start.31 = (bf16[512,512]{0,1:T(8,128)(2,1)}, bf16[512,512]{0,1:T(8,128)(2,1)S(1)}, u32[]{:S(2)}) copy-start(bf16[512,512]{0,1:T(8,128)(2,1)S(1)} %all_gather.43) | copy-start | bytes 1572868
  104.8 46.6 %copy-start.25 = (bf16[2048,512]{1,0:T(8,128)(2,1)S(1)}, bf16[2048,512]{1,0:T(8,128)(2,1)}, u32[]{:S(2)}) copy-start(bf16[2048,512]{1,0:T(8,128)(2,1)} %all-gather.14.cloned.1.call-done) | copy-start | bytes 6291460
  151.4 44.1 %copy-start.30 = (bf16[512,512]{0,1:T(8,128)(2,1)}, bf16[512,512]{0,1:T(8,128)(2,1)S(1)}, u32[]{:S(2)}) copy-start(bf16[512,512]{0,1:T(8,128)(2,1)S(1)} %all_gather.33) | copy-start | bytes 1572868
  218.7 32.4 %copy-start.34 = (bf16[512,512]{1,0:T(8,128)(2,1)S(1)}, bf16[512,512]{1,0:T(8,128)(2,1)}, u32[]{:S(2)}) copy-start(bf16[512,512]{1,0:T(8,128)(2,1)} %all_gather.44) | copy-start | bytes 1572868
  218.7 33.4 %copy-start.36 = (bf16[512,512]{1,0:T(8,128)(2,1)S(1)}, bf16[512,512]{1,0:T(8,128)(2,1)}, u32[]{:S(2)}) copy-start(bf16[512,512]{1,0:T(8,128)(2,1)} %all_gather.37) | copy-start | bytes 1572868
  218.7 141.1 %all-gather.18.cloned.1.call-start = ((), (), s32[]{:S(2)}) async-start(), calls=%async_computation.13 | async-start | bytes 13369344 | tf_op jit(solution)/shard_map/all_gather | solution.py:64
  219.3 241.5 %all-gather.20.cloned.1.call-start = ((), (), s32[]{:S(2)}) async-start(), calls=%async_computation.14 | async-start | bytes 13369344 | tf_op jit(solution)/shard_map/all_gather | solution.py:65
  220.1 344.7 %all-gather.22.cloned.1.call-start = ((), (), s32[]{:S(2)}) async-start(), calls=%async_computation.15 | async-start | bytes 13369344 | tf_op jit(solution)/shard_map/all_gather | solution.py:66
  220.8 439.3 %all-reduce.18.cloned.1.call-start = ((), (), s32[]{:S(2)}) async-start(), calls=%async_computation.26 | async-start | bytes 2097152 | tf_op jit(solution)/shard_map/psum | solution.py:191
  258.9 108.4 %copy-start.74 = (f32[128]{0:T(128)}, f32[128]{0:T(128)S(1)}, u32[]{:S(2)}) copy-start(f32[128]{0:T(128)S(1)} %add_rsqrt_fusion.6) | copy-start | bytes 1540
  258.9 108.4 %copy-start.76 = (f32[128]{0:T(128)}, f32[128]{0:T(128)S(1)}, u32[]{:S(2)}) copy-start(f32[128]{0:T(128)S(1)} %add_rsqrt_fusion.4) | copy-start | bytes 1540
  259.5 201.4 %copy-start.8 = (bf16[128,2048]{1,0:T(8,128)(2,1)}, bf16[128,2048]{1,0:T(8,128)(2,1)S(1)}, u32[]{:S(2)}) copy-start(bf16[128,2048]{1,0:T(8,128)(2,1)S(1)} %get-tuple-element.752) | copy-start | bytes 1572868
  259.5 213.3 %copy-start.10 = (bf16[128,2048]{1,0:T(8,128)(2,1)}, bf16[128,2048]{1,0:T(8,128)(2,1)S(1)}, u32[]{:S(2)}) copy-start(bf16[128,2048]{1,0:T(8,128)(2,1)S(1)} %get-tuple-element.751) | copy-start | bytes 1572868
  460.8 11.9 slice-start
  460.8 11.9 slice-start.1
  586.3 21.9 %slice-start.3 = ((s8[12582912]{0:T(1024)(128)(4,1)}), s8[4194304]{0:T(1024)(128)(4,1)S(1)}, s32[]{:S(2)}) async-start(s8[12582912]{0:T(1024)(128)(4,1)} %bitcast.422), calls=%async_computation.31 | async-start | bytes 8388608
  586.3 21.9 %slice-start.4 = ((s8[12582912]{0:T(1024)(128)(4,1)}), s8[4194304]{0:T(1024)(128)(4,1)S(1)}, s32[]{:S(2)}) async-start(s8[12582912]{0:T(1024)(128)(4,1)} %bitcast.422), calls=%async_computation.32 | async-start | bytes 8388608
  621.6 109.4 %reduce-scatter.12.cloned.1.call-start = ((), (), s32[]{:S(2)}) async-start(), calls=%async_computation.17 | async-start | bytes 1310720 | tf_op jit(solution)/shard_map/reduce_scatter | solution.py:275
  629.5 30.6 %copy-start.17 = (bf16[128,2048]{1,0:T(8,128)(2,1)S(1)}, bf16[128,2048]{1,0:T(8,128)(2,1)}, u32[]{:S(2)}) copy-start(bf16[128,2048]{1,0:T(8,128)(2,1)} %get-tuple-element.723) | copy-start | bytes 1572868
  629.5 30.6 %copy-start.20 = (bf16[128,2048]{1,0:T(8,128)(2,1)S(1)}, bf16[128,2048]{1,0:T(8,128)(2,1)}, u32[]{:S(2)}) copy-start(bf16[128,2048]{1,0:T(8,128)(2,1)} %get-tuple-element.724) | copy-start | bytes 1572868
  629.5 30.6 %copy-start.75 = (f32[128]{0:T(128)S(1)}, f32[128]{0:T(128)}, u32[]{:S(2)}) copy-start(f32[128]{0:T(128)} %copy-done.74) | copy-start | bytes 1540
  629.6 30.6 %copy-start.77 = (f32[128]{0:T(128)S(1)}, f32[128]{0:T(128)}, u32[]{:S(2)}) copy-start(f32[128]{0:T(128)} %copy-done.76) | copy-start | bytes 1540
  694.5 65.2 %reduce-scatter.10.cloned.1.call-start = ((), (), s32[]{:S(2)}) async-start(), calls=%async_computation.16 | async-start | bytes 1310720 | tf_op jit(solution)/shard_map/reduce_scatter | solution.py:275
  711.8 178.2 %all-reduce.16.cloned.1.call-start = ((), (), s32[]{:S(2)}) async-start(), calls=%async_computation.25 | async-start | bytes 4194304 | tf_op jit(solution)/shard_map/psum | solution.py:160
  718.5 45.7 %copy-start.51 = (f32[128,4,128]{0,2,1:T(8,128)S(1)}, f32[128,4,128]{0,2,1:T(8,128)}, u32[]{:S(2)}) copy-start(f32[128,4,128]{0,2,1:T(8,128)} %copy-done.50) | copy-start | bytes 786436
  718.5 45.7 %copy-start.71 = (f32[128]{0:T(128)S(1)}, f32[128]{0:T(128)}, u32[]{:S(2)}) copy-start(f32[128]{0:T(128)} %copy-done.70) | copy-start | bytes 1540
  773.6 187.0 %reduce-scatter.16.cloned.1.call-start = ((), (), s32[]{:S(2)}) async-start(), calls=%async_computation.19 | async-start | bytes 4456448 | tf_op jit(solution)/shard_map/reduce_scatter | solution.py:407
  777.5 211.2 %reduce-scatter.18.cloned.1.call-start = ((), (), s32[]{:S(2)}) async-start(), calls=%async_computation.20 | async-start | bytes 4456448 | tf_op jit(solution)/shard_map/reduce_scatter | solution.py:408
  781.2 314.6 %reduce-scatter.14.cloned.1.call-start = ((), (), s32[]{:S(2)}) async-start(), calls=%async_computation.18 | async-start | bytes 8912896 | tf_op jit(solution)/shard_map/reduce_scatter | solution.py:406
  788.2 415.3 %reduce-scatter.20.cloned.1.call-start = ((), (), s32[]{:S(2)}) async-start(), calls=%async_computation.21 | async-start | bytes 8912896 | tf_op jit(solution)/shard_map/reduce_scatter | solution.py:409
  795.4 12.4 copy-start.9
  795.4 12.4 copy-start.47
  795.5 655.7 %reduce-scatter.22.cloned.1.call-start = ((), (), s32[]{:S(2)}) async-start(), calls=%async_computation.22 | async-start | bytes 26738688 | tf_op jit(solution)/shard_map/reduce_scatter | solution.py:410
  825.7 872.6 %reduce-scatter.24.cloned.1.call-start = ((), (), s32[]{:S(2)}) async-start(), calls=%async_computation.23 | async-start | bytes 26738688 | tf_op jit(solution)/shard_map/reduce_scatter | solution.py:411
  854.0 12.5 copy-start.29
  854.0 1091.3 %reduce-scatter.26.cloned.1.call-start = ((), (), s32[]{:S(2)}) async-start(), calls=%async_computation.24 | async-start | bytes 26738688 | tf_op jit(solution)/shard_map/reduce_scatter | solution.py:412
  883.5 71.5 %copy-start.15 = (f32[128,2048]{1,0:T(8,128)S(1)}, f32[128,2048]{1,0:T(8,128)}, u32[]{:S(2)}) copy-start(f32[128,2048]{1,0:T(8,128)} %copy-done.13) | copy-start | bytes 3145732
  883.5 71.5 %copy-start.18 = (bf16[128,2048]{1,0:T(8,128)(2,1)S(1)}, bf16[128,2048]{1,0:T(8,128)(2,1)}, u32[]{:S(2)}) copy-start(bf16[128,2048]{1,0:T(8,128)(2,1)} %get-tuple-element.723) | copy-start | bytes 1572868
  (61 other events, 198.4 us)
Sparse Core Ops, SparseCore 0:
  10.2 44.1 all-gather.9
  56.6 40.6 all-gather.13
  99.6 61.0 all-gather.11
  162.6 50.6 all-gather.15
  218.9 38.2 all-reduce.19
  259.3 100.4 all-gather.17
  362.1 98.6 all-gather.19
  462.9 101.8 all-gather.21
  621.8 38.2 all-reduce.17
  694.6 36.3 reduce-scatter.11
  733.9 25.7 reduce-scatter.9
  773.7 61.5 all-reduce.15
  839.7 72.9 reduce-scatter.15
  917.0 71.6 reduce-scatter.17
  993.2 102.4 reduce-scatter.13
  1100.2 103.1 reduce-scatter.19
  1208.0 243.1 reduce-scatter.21
  1455.7 242.5 reduce-scatter.23
  1703.0 242.2 reduce-scatter.25
where the time goes:
time: 1960 us; the launch traced here: 1950 us
  waiting for transfers between devices  1340 us (68%)
  blocking collectives  240 us (12%)
  matrix products  240 us (12%)
  local copies, waits for them, and re-layouts  61.3 us (3%)
  other arithmetic  45.7 us (2%)
    reduce_scatter x1, waiting for transfers between devices, on_device(): lax.psum_scatter(totals[8], ('dp', 'ctx'), scatter_dimension=0, tiled=True)  248 us
    reduce_scatter x1, waiting for transfers between devices, on_device(): lax.psum_scatter(totals[9], ('dp', 'ctx'), scatter_dimension=0, tiled=True)  247 us
    reduce_scatter x1, waiting for transfers between devices, on_device(): lax.psum_scatter(totals[10], ('dp', 'ctx'), scatter_dimension=1, tiled=True)  247 us
    reduce_scatter x1, waiting for transfers between devices, on_device(): lax.psum_scatter(totals[7], ('dp', 'ctx'), scatter_dimension=1, tiled=True)  108 us
    reduce_scatter x1, waiting for transfers between devices, on_device(): lax.psum_scatter(totals[4], ('dp', 'ctx'), scatter_dimension=0, tiled=True)  107 us
    dot_general x14, matrix products, dot_tn(): lax.dot_general(left, right, (((0,), (0,)), ((), ())), preferred_element_...  106 us
    all_gather x1, waiting for transfers between devices, micro_pass(): lax.all_gather(shards[8], ('dp', 'ctx'), axis=0, tiled=True)  100 us
    all_gather x1, waiting for transfers between devices, micro_pass(): lax.all_gather(shards[9], ('dp', 'ctx'), axis=0, tiled=True)  93.5 us
  transfers between devices with their start and end apart: 19, of which 14 were waited for; matrix products, arithmetic and copies ran while one was open for 12% of the time, Pallas kernels for 0%

commit v1 on v0

--- a/solution.py
+++ b/solution.py
@@ -1,10 +1,979 @@
+import functools
+
 import jax
 import jax.numpy as jnp
 from jax import lax
+from jax.experimental import pallas as pl
+from jax.experimental.pallas import tpu as pltpu
 from jax.sharding import PartitionSpec as P
 
 eps_norm = 1e-06
 rope_base = 1000000.0
+MESH = pl.DeviceIdType.MESH
+f32 = jnp.float32
+bf16 = jnp.bfloat16
+DP, CTX, MP = "dp", "ctx", "mp"
+CORE, LOW, ACROSS, DIAG, HIGH, ACROSS_X = range(6)
+PIECES = ((0, 0), (0, 1), (1, 0), (1, 1))
+
+
+def flip(value, bit):
+    return 1 - value if bit else value
+
+
+def place():
+    dp = lax.axis_index(DP)
+    ctx = lax.axis_index(CTX)
+    return {
+        DP: dp,
+        CTX: ctx,
+        "y": lax.axis_index(MP),
+        "x": dp // 2,
+        "c": dp % 2,
+        "zh": ctx // 2,
+        "zl": ctx % 2,
+    }
+
+
+def run_start(at, dx, dzh, dc, ctx_count, block):
+    start = ((flip(at["x"], dx) * 2 + flip(at["c"], dc)) * ctx_count + flip(at["zh"], dzh) * 2) * block
+    return pl.multiple_of(start, 2 * block)
+
+
+def finish(copies):
+    for copy in copies:
+        copy.wait()
+
+
+def nn(left, right):
+    return lax.dot_general(left, right, (((1,), (0,)), ((), ())), preferred_element_type=f32)
+
+
+def nt(left, right):
+    return lax.dot_general(left, right, (((1,), (1,)), ((), ())), preferred_element_type=f32)
+
+
+def tn(left, right):
+    return lax.dot_general(left, right, (((0,), (0,)), ((), ())), preferred_element_type=f32)
+
+
+def root_scale(values):
+    return lax.rsqrt(jnp.mean(values * values, axis=-1, keepdims=True) + eps_norm)
+
+
+def turn(values, cosine, sine):
+    return values * cosine + pltpu.roll(values, values.shape[-1] // 2, 1) * sine
+
+
+def turn_back(values, cosine, sine):
+    return values * cosine + pltpu.roll(values * sine, values.shape[-1] // 2, 1)
+
+
+def pair_rows(ref, base, part, span):
+    far = base + 2 * part
+    return jnp.concatenate(
+        [ref[pl.ds(base, part), :][:, span[0] : span[1]], ref[pl.ds(far, part), :][:, span[0] : span[1]]], axis=0
+    )
+
+
+def allowed_pairs(at, n, m, part, heads, extra):
+    def fold(index, size, times):
+        for k in range(times - 1, 0, -1):
+            index = jnp.where(index >= k * size, index - k * size, index)
+        return index
+
+    row = lax.broadcasted_iota(jnp.int32, (heads * 2 * part, 4 * part), 0)
+    col = lax.broadcasted_iota(jnp.int32, (heads * 2 * part, 4 * part), 1)
+    near = at["zl"] * part
+    far = (1 - at["zl"]) * part
+    row = fold(row, 2 * part, heads)
+    query = jnp.where(row < part, row + near, row - part + far) + at["zh"] * 2 * part
+    inner = fold(col, 2 * part, 2)
+    key = jnp.where(inner < part, inner + near, inner - part + far)
+    key = key + jnp.where(col < 2 * part, at["zh"], 1 - at["zh"]) * (2 * part)
+    query, key = query.astype(f32), key.astype(f32)
+    spot = jnp.concatenate([extra[n * 4 + m, 1], extra[n * 4 + 2 + m, 1]] * heads, axis=0)[:, :1]
+    return (key <= query) & (key >= query - spot)
+
+
+def stack_heads(ref, base, part, head):
+    heads = ref.shape[1] // head
+    return jnp.concatenate([pair_rows(ref, base, part, (h * head, (h + 1) * head)) for h in range(heads)], axis=0)
+
+
+def unstack(ref, base, part, head, values):
+    heads = ref.shape[1] // head
+    for h in range(heads):
+        top = 2 * part * h
+        ref[pl.ds(base, part), pl.ds(h * head, head)] = values[top : top + part].astype(ref.dtype)
+        ref[pl.ds(base + 2 * part, part), pl.ds(h * head, head)] = values[top + part : top + 2 * part].astype(ref.dtype)
+
+
+def partners(at):
+    return (
+        {DP: at[DP] + 1 - 2 * at["c"]},
+        {CTX: at[CTX] + 1 - 2 * at["zl"]},
+        {MP: 1 - at["y"]},
+    )
+
+
+class Lines:
+    def __init__(self, send, recv):
+        self.send, self.recv, self.used, self.open = send, recv, 0, []
+
+    def start(self, source, target, device):
+        copy = pltpu.make_async_remote_copy(
+            src_ref=source,
+            dst_ref=target,
+            send_sem=self.send.at[self.used],
+            recv_sem=self.recv.at[self.used],
+            device_id=device,
+            device_id_type=MESH,
+        )
+        copy.start()
+        self.used += 1
+        self.open.append(copy)
+        return copy
+
+    def close(self):
+        self.settle(list(self.open))
+
+    def settle(self, copies):
+        for copy in copies:
+            copy.wait_send()
+        self.open = [copy for copy in self.open if all(copy is not done for done in copies)]
+
+
+class Moves:
+    def __init__(self, sems):
+        self.sems, self.used, self.open = sems, 0, []
+
+    def start(self, source, target):
+        copy = pltpu.make_async_copy(source, target, self.sems.at[self.used])
+        copy.start()
+        self.used += 1
+        return copy
+
+    def save(self, source, target):
+        self.open.append(self.start(source, target))
+
+    def close(self):
+        finish(self.open)
+
+
+def arrive(copies):
+    for copy in copies:
+        copy.wait_recv()
+
+
+def neighbours(at):
+    core, low, across = partners(at)
+    return {
+        CORE: core,
+        LOW: low,
+        ACROSS: across,
+        DIAG: {**core, **low},
+        HIGH: {CTX: at[CTX] + 2 - 4 * at["zh"]},
+        ACROSS_X: {DP: at[DP] + 2 - 4 * at["x"]},
+    }
+
+
+def meet_all(near, names):
+    barrier = pltpu.get_barrier_semaphore()
+    for name in names:
+        pl.semaphore_signal(barrier, inc=1, device_id=near[name], device_id_type=MESH)
+    pl.semaphore_wait(barrier, len(names))
+
+
+class Env:
+    def __init__(self, at, near, lines, moves, ctx_count, block):
+        self.at, self.near, self.lines, self.moves = at, near, lines, moves
+        self.ctx_count, self.block = ctx_count, block
+
+
+class Weight:
+    def __init__(self, env, shard, target, by_rows, low, size):
+        self.env, self.shard, self.target, self.by_rows, self.low, self.size = env, shard, target, by_rows, low, size
+        self.over_z, self.own_x, self.far_x = [None, None], [None, None], [None, None]
+
+    def mine(self):
+        at, ctx_count, block = self.env.at, self.env.ctx_count, self.env.block
+        spot = pl.ds(pl.multiple_of((at[DP] * ctx_count + at[CTX]) * block, block), block)
+        return self.target.at[spot, pl.ds(self.low, self.size)] if self.by_rows else self.target.at[:, spot]
+
+    def run(self, dx, dzh, dc):
+        spot = pl.ds(run_start(self.env.at, dx, dzh, dc, self.env.ctx_count, self.env.block), 2 * self.env.block)
+        return self.target.at[spot, pl.ds(self.low, self.size)] if self.by_rows else self.target.at[:, spot]
+
+    def cut(self, dc, dzl):
+        at = self.env.at
+        start = pl.multiple_of((flip(at["c"], dc) * 2 + flip(at["zl"], dzl)) * self.size, 128)
+        return self.shard.at[:, pl.ds(start, self.size)] if self.by_rows else self.shard.at[pl.ds(start, self.size), :]
+
+    def exchange(self):
+        near, lines = self.env.near, self.env.lines
+        self.local = self.env.moves.start(self.cut(0, 0), self.mine())
+        self.got = [
+            lines.start(self.cut(dc, dzl), self.mine(), near[name])
+            for dc, dzl, name in ((0, 1, LOW), (1, 0, CORE), (1, 1, DIAG))
+        ]
+
+    def ready(self):
+        self.local.wait()
+        arrive(self.got)
+
+    def send_z(self, dc):
+        self.over_z[dc] = self.env.lines.start(self.run(0, 0, dc), self.run(0, 0, dc), self.env.near[HIGH])
+
+    def send_x(self, dc):
+        self.own_x[dc] = self.env.lines.start(self.run(0, 0, dc), self.run(0, 0, dc), self.env.near[ACROSS_X])
+
+    def pass_x(self, dc):
+        self.over_z[dc].wait_recv()
+        self.far_x[dc] = self.env.lines.start(self.run(0, 1, dc), self.run(0, 1, dc), self.env.near[ACROSS_X])
+
+    def complete(self):
+        arrive(self.own_x + self.far_x)
+
+
+class Gains(Weight):
+    def mine(self):
+        return self.target.at[self.env.at[DP] * self.env.ctx_count + self.env.at[CTX]]
+
+    def run(self, dx, dzh, dc):
+        at = self.env.at
+        return self.target.at[
+            pl.ds((flip(at["x"], dx) * 2 + flip(at["c"], dc)) * self.env.ctx_count + flip(at["zh"], dzh) * 2, 2)
+        ]
+
+    def cut(self, dc, dzl):
+        return self.shard
+
+
+def tables(extra, n):
+    packed = extra[n, 0]
+    turned = pltpu.roll(packed, packed.shape[1] // 2, 1)
+    first = lax.broadcasted_iota(jnp.int32, packed.shape, 1) < packed.shape[1] // 2
+    return jnp.where(first, packed, turned), jnp.where(first, -turned, packed)
+
+
+def forward_kernel(
+    ctx_count, block, head,
+    x_hbm, c_hbm, extra_hbm, gain_hbm, wq, wk, wv, wo, wg, wu, wd,
+    a_out, raw_out, q_out, kv_out, kvp_out, o_out, lse_out, h_out, b_out, z_out, gu_out, c_out, extra_out, gains_out,
+    wqkv_out, wo_out, wgu_out, wd_out,
+    x, extra, gain_all, wqkv, w_o, wgu, w_d, a, raw, q, kv, kvp, o, lse, from_core, kept, second_a, second_b, from_z, from_y, last_a, last_b,
+    h, b_all, z, gu, c, gains, send, recv, local,
+):
+    at = place()
+    near = neighbours(at)
+    lines, moves = Lines(send, recv), Moves(local)
+    env = Env(at, near, lines, moves, ctx_count, block)
+    part, width = x.shape[1], x.shape[2]
+    q_width = q.shape[1]
+    hidden = z.shape[1]
+    rows = 2 * part
+    meet_all(near, (CORE, LOW, ACROSS, DIAG, HIGH, ACROSS_X))
+
+    seq = [flip(at["y"], ds) for ds in (0, 1)]
+    x_low = lines.start(x_hbm.at[seq[0]], x.at[2], near[LOW])
+    e_low = lines.start(extra_hbm.at[0], extra.at[2], near[LOW])
+    units = (
+        Weight(env, wq, wqkv, True, 0, q_width),
+        Weight(env, wk, wqkv, True, q_width, head),
+        Weight(env, wv, wqkv, True, q_width + head, head),
+    )
+    scale = Gains(env, gain_hbm, gain_all, True, 0, 0)
+    for unit in (scale, *units):
+        unit.exchange()
+    x_core = [lines.start(x_hbm.at[seq[ds]], x.at[4 + ds], near[CORE]) for ds in (0, 1)]
+    e_core = lines.start(extra_hbm, extra.at[pl.ds(4, 2)], near[CORE])
+    x_own = [moves.start(x_hbm.at[seq[ds]], x.at[ds]) for ds in (0, 1)]
+    e_own = moves.start(extra_hbm, extra.at[pl.ds(0, 2)])
+    for unit in (scale, *units):
+        unit.ready()
+    in_qkv = Weight(env, None, wqkv, True, 0, wqkv.shape[1])
+    for dc in (0, 1):
+        scale.send_z(dc)
+        scale.send_x(dc)
+        in_qkv.send_z(dc)
+        in_qkv.send_x(dc)
+    w_out = Weight(env, wo, w_o, False, 0, q_width)
+    w_gate = Weight(env, wg, wgu, True, 0, hidden)
+    w_up = Weight(env, wu, wgu, True, hidden, hidden)
+    w_down = Weight(env, wd, w_d, False, 0, hidden)
+    w_out.exchange()
+    w_gate.exchange()
+    x_far, x_across = share(near, lines, x, x_low)
+    e_far, e_across = share(near, lines, extra, e_low)
+    w_up.exchange()
+    w_down.exchange()
+    x_far.append(pass_on(near, lines, x, x_across))
+    e_far.append(pass_on(near, lines, extra, e_across))
+    for dc in (0, 1):
+        scale.pass_x(dc)
+        in_qkv.pass_x(dc)
+    w_out.ready()
+    for dc in (0, 1):
+        w_out.send_z(dc)
+        w_out.send_x(dc)
+    w_gate.ready()
+    w_gate.send_z(0)
+    scale.complete()
+    gains[...] = jnp.zeros_like(gains)
+    ranks = gain_all.shape[0]
+    small = gain_all[0, 2:4, :]
+    for n in range(ranks):
+        gains[0:2, n * block : (n + 1) * block] = gain_all[n, 0:2, :]
+        if n:
+            small = small + gain_all[n, 2:4, :]
+    gains[2:4, 0:head] = small
+
+    finish(x_own)
+    arrive(x_core + x_far)
+    e_own.wait()
+    arrive([e_core, *e_far])
+    h[...] = x[0].astype(f32)
+
+    @pl.loop(0, 8)
+    def _(n):
+        wide = x[n].astype(f32)
+        span = pl.ds(pl.multiple_of(n * part, part), part)
+        a[span, :] = (wide * root_scale(wide) * gains[0:1, :]).astype(bf16)
+
+    in_qkv.complete()
+    moves.save(wqkv, wqkv_out)
+    gain_q = gains[2:3, 0:head]
+    gain_k = gains[3:4, 0:head]
+
+    @pl.loop(0, 4)
+    def _(m):
+        big = pl.ds(pl.multiple_of(m * rows, rows), rows)
+        product = nn(a[big, :], wqkv[...])
+        raw[big, :] = product[:, : q_width + head]
+        for half in (0, 1):
+            n = 2 * m + half
+            span = pl.ds(pl.multiple_of(n * part, part), part)
+            cos, sin = tables(extra, n)
+            piece = product[half * part : (half + 1) * part]
+            for j in range(q_width // head):
+                u = piece[:, j * head : (j + 1) * head]
+                q[span, pl.ds(j * head, head)] = turn(u * root_scale(u) * gain_q, cos, sin).astype(bf16)
+            u = piece[:, q_width : q_width + head]
+            kv[span, pl.ds(0, head)] = turn(u * root_scale(u) * gain_k, cos, sin).astype(bf16)
+            kv[span, pl.ds(head, head)] = piece[:, q_width + head :].astype(bf16)
+
+    kv_far = lines.start(kv, kvp, near[HIGH])
+    for source, target in ((a, a_out), (raw, raw_out), (q, q_out), (kv, kv_out), (extra, extra_out), (gains, gains_out)):
+        moves.save(source, target)
+    for dc in (0, 1):
+        w_out.pass_x(dc)
+    for dc in (0, 1):
+        w_gate.send_x(dc)
+    kv_far.wait_recv()
+    w_gate.send_z(1)
+    c_own = [moves.start(c_hbm.at[seq[ds]], c.at[ds]) for ds in (0, 1)]
+    c_core = [lines.start(c_hbm.at[seq[ds]], c.at[4 + ds], near[CORE]) for ds in (0, 1)]
+    c_low = lines.start(c_hbm.at[seq[0]], c.at[2], near[LOW])
+    w_up.ready()
+    for dc in (0, 1):
+        w_up.send_z(dc)
+        w_up.send_x(dc)
+    moves.save(kvp, kvp_out)
+    scaling = head ** (-0.5)
+
+    @pl.loop(0, 2)
+    def _(n):
+        @pl.loop(0, 2)
+        def _(m):
+            base = pl.multiple_of(n * (4 * part) + m * part, part)
+            keys = jnp.concatenate([pair_rows(kv, base, part, (0, head)), pair_rows(kvp, base, part, (0, head))], axis=0)
+            values = jnp.concatenate(
+                [pair_rows(kv, base, part, (head, 2 * head)), pair_rows(kvp, base, part, (head, 2 * head))], axis=0
+            )
+            allowed = allowed_pairs(at, n, m, part, q_width // head, extra)
+            scores = jnp.where(allowed, nt(stack_heads(q, base, part, head), keys) * scaling, -jnp.inf)
+            peak = jnp.max(scores, axis=-1, keepdims=True)
+            weights = jnp.exp(scores - peak)
+            total = jnp.sum(weights, axis=-1, keepdims=True)
+            mixed = nn(weights.astype(bf16), values) / total
+            unstack(o, base, part, head, mixed)
+            unstack(lse, base, part, head, jnp.broadcast_to(peak + jnp.log(total), mixed.shape))
+
+    moves.save(o, o_out)
+    moves.save(lse, lse_out)
+    w_out.complete()
+    moves.save(w_o, wo_out)
+    out = x
+    lines.settle([*x_far, x_across])
+
+    def project(first):
+        @pl.loop(0, 4)
+        def _(m):
+            n = first + m
+            span = pl.ds(pl.multiple_of(n * part, part), part)
+            out[n] = nn(o[span, :], w_o[...]).astype(bf16)
+
+    project(4)
+    sent = {k: lines.start(out.at[4 + k], from_core.at[k], near[CORE]) for k in (3, 1, 2, 0)}
+    project(0)
+
+    def pump_gate():
+        for dc in (0, 1):
+            w_gate.pass_x(dc)
+        w_down.ready()
+        for dc in (0, 1):
+            w_down.send_z(dc)
+            w_down.send_x(dc)
+        return share(near, lines, c, c_low)
+
+    sums, (c_far, c_across) = sum_lines(near, lines, out, sent, from_core, kept, second_a, second_b, from_z, from_y, last_a, last_b, pump_gate)
+    h[...] = h[...] + sums
+    moves.save(h, h_out)
+    wide = h[...]
+    b_all[0] = (wide * root_scale(wide) * gains[1:2, :]).astype(bf16)
+
+    def pump_up():
+        for dc in (0, 1):
+            w_up.pass_x(dc)
+        c_far.append(pass_on(near, lines, c, c_across))
+
+    spread_lines(near, lines, b_all, from_z.shape[2], pump_up)
+    moves.save(b_all, b_out)
+
+    w_gate.complete()
+
+    w_up.complete()
+    moves.save(wgu, wgu_out)
+
+    @pl.loop(0, 4)
+    def _(m):
+        span = pl.ds(pl.multiple_of(m * rows, rows), rows)
+        b = pair(b_all, m)
+        g = nn(b, wgu[:, 0:hidden])
+        u = nn(b, wgu[:, hidden : 2 * hidden])
+        gu[span, pl.ds(0, hidden)] = g.astype(bf16)
+        gu[span, pl.ds(hidden, hidden)] = u.astype(bf16)
+        z[span, :] = (g * jax.nn.sigmoid(g) * u).astype(bf16)
+
+    moves.save(z, z_out)
+    moves.save(gu, gu_out)
+    finish(c_own)
+    arrive(c_core + c_far)
+    moves.save(c, c_out)
+    for dc in (0, 1):
+        w_down.pass_x(dc)
+    w_down.complete()
+    moves.save(w_d, wd_out)
+    lines.close()
+    moves.close()
+
+
+def share(near, lines, ref, low):
+    low.wait_recv()
+    across = lines.start(ref.at[2], ref.at[3], near[ACROSS])
+    return [lines.start(ref.at[2], ref.at[6], near[CORE])], across
+
+
+def pass_on(near, lines, ref, across):
+    across.wait_recv()
+    return lines.start(ref.at[3], ref.at[7], near[CORE])
+
+
+def pair(ref, m):
+    return jnp.concatenate([ref[2 * m], ref[2 * m + 1]], axis=0)
+
+
+def sum_lines(near, lines, part, first, from_core, kept, second_a, second_b, from_z, from_y, last_a, last_b, pump):
+    width, cut = part.shape[2], from_z.shape[2]
+    a, b = pl.ds(0, cut), pl.ds(cut, width - cut)
+
+    def total(k):
+        first[k].wait_recv()
+        return part[k].astype(f32) + from_core[k].astype(f32)
+
+    kept[2] = total(3).astype(bf16)
+    y1 = lines.start(kept.at[2, :, b], from_y.at[1], near[ACROSS])
+    z1 = lines.start(kept.at[2, :, a], from_z.at[1], near[LOW])
+    kept[0] = total(1).astype(bf16)
+    y0 = lines.start(kept.at[0, :, b], from_y.at[0], near[ACROSS])
+    kept[1] = total(2).astype(bf16)
+    z0 = lines.start(kept.at[1, :, a], from_z.at[0], near[LOW])
+    y1.wait_recv()
+    second_b[...] = (kept[1, :, b].astype(f32) + from_y[1].astype(f32)).astype(bf16)
+    z2 = lines.start(second_b, last_b, near[LOW])
+    z1.wait_recv()
+    second_a[...] = (kept[0, :, a].astype(f32) + from_z[1].astype(f32)).astype(bf16)
+    y2 = lines.start(second_a, last_a, near[ACROSS])
+    extra = pump()
+    mine = total(0)
+    arrive((z0, y0, y2, z2))
+    lines.settle([*first.values(), z1, y1, y0, z0, y2, z2])
+    left = mine[:, :cut] + from_z[0].astype(f32) + last_a[...].astype(f32)
+    right = mine[:, cut:] + from_y[0].astype(f32) + last_b[...].astype(f32)
+    return jnp.concatenate([left, right], axis=1), extra
+
+
+def spread_lines(near, lines, out, cut, pump):
+    width = out.shape[2]
+    a, b = pl.ds(0, cut), pl.ds(cut, width - cut)
+    zb = lines.start(out.at[0, :, b], out.at[2, :, b], near[LOW])
+    ya = lines.start(out.at[0, :, a], out.at[1, :, a], near[ACROSS])
+    yb = lines.start(out.at[0, :, b], out.at[1, :, b], near[ACROSS])
+    za = lines.start(out.at[0, :, a], out.at[2, :, a], near[LOW])
+    c0 = lines.start(out.at[0], out.at[4], near[CORE])
+    ya.wait_recv()
+    zc = lines.start(out.at[1, :, a], out.at[3, :, a], near[LOW])
+    zb.wait_recv()
+    yc = lines.start(out.at[2, :, b], out.at[3, :, b], near[ACROSS])
+    yb.wait_recv()
+    c1 = lines.start(out.at[1], out.at[5], near[CORE])
+    za.wait_recv()
+    c2 = lines.start(out.at[2], out.at[6], near[CORE])
+    zc.wait_recv()
+    yc.wait_recv()
+    c3 = lines.start(out.at[3], out.at[7], near[CORE])
+    pump()
+    arrive((c0, c1, c2, c3))
+    return [ya, zb, yb, za, c0, zc, yc, c1, c2, c3]
+
+
+class Grad:
+    def __init__(self, env, work, by_rows, over_x, over_z, outs):
+        self.env, self.work, self.by_rows, self.outs = env, work, by_rows, outs
+        self.from_x, self.from_z = over_x, over_z
+        self.x, self.z, self.last, self.local = {}, {}, [], []
+
+    def index(self, dx, dzh, dc):
+        spot = pl.ds(run_start(self.env.at, dx, dzh, dc, self.env.ctx_count, self.env.block), 2 * self.env.block)
+        return (spot, slice(None)) if self.by_rows else (slice(None), spot)
+
+    def send_x(self, dzh, dc):
+        self.x[dzh, dc] = self.env.lines.start(
+            self.work.at[self.index(1, dzh, dc)], self.from_x.at[2 * dzh + dc], self.env.near[ACROSS_X]
+        )
+
+    def pass_z(self, dc):
+        self.x[1, dc].wait_recv()
+        spot = self.index(0, 1, dc)
+        self.work[spot] = (self.work[spot].astype(f32) + self.from_x[2 + dc].astype(f32)).astype(bf16)
+        self.z[dc] = self.env.lines.start(self.work.at[spot], self.from_z.at[dc], self.env.near[HIGH])
+
+    def deliver(self, dc):
+        at, block = self.env.at, self.env.block
+        self.x[0, dc].wait_recv()
+        self.z[dc].wait_recv()
+        spot = self.index(0, 0, dc)
+        self.work[spot] = (
+            self.work[spot].astype(f32) + self.from_x[dc].astype(f32) + self.from_z[dc].astype(f32)
+        ).astype(bf16)
+        slot = at["c"] * 2 + at["zl"]
+        for dzl, name in ((1, (LOW, DIAG)[dc]), (0, (None, CORE)[dc])):
+            start = run_start(at, 0, 0, dc, self.env.ctx_count, block) + flip(at["zl"], dzl) * block
+            mine = pl.ds(pl.multiple_of(start, block), block)
+            for out, low, size in self.outs:
+                there = pl.ds(pl.multiple_of(slot * size, 128), size)
+                if self.by_rows:
+                    source, target = self.work.at[mine, pl.ds(low, size)], out.at[:, there]
+                else:
+                    source, target = self.work.at[:, mine], out.at[there, :]
+                if name is None:
+                    self.local.append(self.env.moves.start(source, target))
+                else:
+                    self.last.append(self.env.lines.start(source, target, self.env.near[name]))
+
+    def finish(self):
+        arrive(self.last)
+        finish(self.local)
+
+
+def eighths_of(unit, dx, make):
+    @pl.loop(0, 2)
+    def _(dzh):
+        @pl.loop(0, 2)
+        def _(dc):
+            at, count = unit.env.at, unit.env.ctx_count
+            near_zh = at["zh"] + dzh - 2 * at["zh"] * dzh
+            near_c = at["c"] + dc - 2 * at["c"] * dc
+            start = ((flip(at["x"], dx) * 2 + near_c) * count + near_zh * 2) * unit.env.block
+            spot = pl.ds(pl.multiple_of(start, 2 * unit.env.block), 2 * unit.env.block)
+            value = make(spot).astype(bf16)
+            if unit.by_rows:
+                unit.work[spot, :] = value
+            else:
+                unit.work[:, spot] = value
+
+
+def columns(ref, run):
+    block = ref[:, :, run]
+    return block.reshape(block.shape[0] * block.shape[1], block.shape[2])
+
+
+def backward_kernel(
+    ctx_count, block, head,
+    x_hbm, a_hbm, raw_hbm, q_hbm, kv_hbm, kvp_hbm, o_hbm, lse_hbm, h_hbm, b_hbm, z_hbm, gu_hbm, c_hbm, extra_hbm, gains_hbm,
+    wqkv_hbm, wo_hbm, wgu_hbm, wd_hbm,
+    out_hbm, in_hbm, g_query, g_key, g_value, g_out, g_gate, g_up, g_down, small_out,
+    c, wd, z, gu, wgu, b, q, kv, kvp, o, lse, raw, extra, gains, wqkv, wo, h, dh, x_mine, dq, dkv, dkvp, got, do, dqkv,
+    work_d, work_o, work_q, rx_d, rz_d, rx_g, rz_g, rx_o, rz_o, rx_q, rz_q,
+    from_core, kept, second_a, second_b, from_z, from_y, last_a, last_b, own_out, own_in, sums, small, rx_s, rz_s, ry_s,
+    send, recv, local, ready, done,
+):
+    at = place()
+    near = neighbours(at)
+    lines, moves = Lines(send, recv), Moves(local)
+    env = Env(at, near, lines, moves, ctx_count, block)
+    part, width = c.shape[1], c.shape[2]
+    q_width = q.shape[1]
+    hidden = z.shape[1]
+    rows = 2 * part
+    scaling = head ** (-0.5)
+    fetch = moves.start
+    get_z, get_c, get_d, get_gu = fetch(z_hbm, z), fetch(c_hbm, c), fetch(wd_hbm, wd), fetch(gu_hbm, gu)
+    get_w, get_b = fetch(wgu_hbm, wgu), fetch(b_hbm, b)
+    get_more = [fetch(*p) for p in ((h_hbm, h), (gains_hbm, gains), (wo_hbm, wo), (o_hbm, o))]
+    get_rest = [
+        fetch(*p)
+        for p in ((q_hbm, q), (kv_hbm, kv), (kvp_hbm, kvp), (lse_hbm, lse), (raw_hbm, raw), (extra_hbm, extra), (wqkv_hbm, wqkv))
+    ]
+    get_x = fetch(x_hbm.at[at["y"]], x_mine)
+    meet_all(near, (CORE, LOW, ACROSS, DIAG, HIGH, ACROSS_X))
+    down = Grad(env, work_d, False, rx_d, rz_d, ((g_down, 0, hidden),))
+    gate = Grad(env, wgu, True, rx_g, rz_g, ((g_gate, 0, hidden), (g_up, hidden, hidden)))
+    outward = Grad(env, work_o, False, rx_o, rz_o, ((g_out, 0, q_width),))
+    inward = Grad(env, work_q, True, rx_q, rz_q, ((g_query, 0, q_width), (g_key, q_width, head), (g_value, q_width + head, head)))
+
+    get_z.wait()
+    get_c.wait()
+    eighths_of(down, 1, lambda run: tn(z[...], columns(c, run)))
+    for dc in (0, 1):
+        down.send_x(1, dc)
+    eighths_of(down, 0, lambda run: tn(z[...], columns(c, run)))
+    get_d.wait()
+    get_gu.wait()
+    dh[...] = c[0].astype(f32)
+
+    @pl.loop(0, 4)
+    def _(m):
+        span = pl.ds(pl.multiple_of(m * rows, rows), rows)
+        dz = nt(pair(c, m), wd[...])
+        g = gu[span, pl.ds(0, hidden)].astype(f32)
+        u = gu[span, pl.ds(hidden, hidden)].astype(f32)
+        s = jax.nn.sigmoid(g)
+        gu[span, pl.ds(0, hidden)] = (dz * u * s * (1.0 + g * (1.0 - s))).astype(bf16)
+        gu[span, pl.ds(hidden, hidden)] = (dz * g * s).astype(bf16)
+
+    get_w.wait()
+
+    def spill(first, source, weight, back):
+        @pl.loop(0, 2)
+        def _(m):
+            n = first // 2 + m
+            span = pl.ds(pl.multiple_of(n * rows, rows), rows)
+            product = (nt if back else nn)(source[span, :], weight[...]).astype(bf16)
+            c[2 * n] = product[:part]
+            c[2 * n + 1] = product[part:]
+
+    def to_core():
+        return {k: lines.start(c.at[4 + k], from_core.at[k], near[CORE]) for k in (3, 1, 2, 0)}
+
+    spill(4, gu, wgu, True)
+    sent = to_core()
+    spill(0, gu, wgu, True)
+    for dc in (0, 1):
+        down.pass_z(dc)
+    get_b.wait()
+    eighths_of(gate, 1, lambda run: tn(columns(b, run), gu[...]))
+    for dc in (0, 1):
+        gate.send_x(1, dc)
+    eighths_of(gate, 0, lambda run: tn(columns(b, run), gu[...]))
+    for device in (CORE, LOW, ACROSS):
+        pl.semaphore_signal(ready, inc=1, device_id=near[device], device_id_type=MESH)
+    finish(get_more)
+
+    def pump_down():
+        for dc in (0, 1):
+            down.send_x(0, dc)
+        for dc in (0, 1):
+            gate.send_x(0, dc)
+
+    db, _ = sum_lines(near, lines, c, sent, from_core, kept, second_a, second_b, from_z, from_y, last_a, last_b, pump_down)
+    wide = h[...]
+    r = root_scale(wide)
+    n_m = wide * r
+    sums[1:2, :] = jnp.sum(db * n_m, axis=0, keepdims=True)
+    t = db * gains[1:2, :]
+    middle = dh[...] + r * (t - n_m * jnp.mean(t * n_m, axis=-1, keepdims=True))
+    dh[...] = middle
+    pl.semaphore_wait(ready, 3)
+    b[0] = middle.astype(bf16)
+    spread = spread_lines(near, lines, b, from_z.shape[2], lambda: None)
+    gate.pass_z(0)
+
+    @pl.loop(0, 4)
+    def _(m):
+        span = pl.ds(pl.multiple_of(m * rows, rows), rows)
+        do[span, :] = nt(pair(b, m), wo[...]).astype(bf16)
+
+    eighths_of(outward, 1, lambda run: tn(o[...], columns(b, run)))
+    for dzh, dc in ((1, 0), (1, 1), (0, 0), (0, 1)):
+        outward.send_x(dzh, dc)
+    eighths_of(outward, 0, lambda run: tn(o[...], columns(b, run)))
+    lines.settle(spread)
+    get_a = fetch(a_hbm, b)
+    finish(get_rest)
+
+    @pl.loop(0, 2)
+    def _(n):
+        @pl.loop(0, 2)
+        def _(m):
+            base = pl.multiple_of(n * (4 * part) + m * part, part)
+            query = stack_heads(q, base, part, head)
+            mixed = stack_heads(o, base, part, head)
+            grad = stack_heads(do, base, part, head)
+            level = stack_heads(lse, base, part, head)[:, :1]
+            keys = jnp.concatenate([pair_rows(kv, base, part, (0, head)), pair_rows(kvp, base, part, (0, head))], axis=0)
+            values = jnp.concatenate(
+                [pair_rows(kv, base, part, (head, 2 * head)), pair_rows(kvp, base, part, (head, 2 * head))], axis=0
+            )
+            allowed = allowed_pairs(at, n, m, part, q_width // head, extra)
+            probs = jnp.where(allowed, jnp.exp(jnp.where(allowed, nt(query, keys) * scaling - level, 0.0)), 0.0)
+            dv = tn(probs.astype(bf16), grad)
+            row_dot = jnp.sum(grad.astype(f32) * mixed.astype(f32), axis=-1, keepdims=True)
+            ds = (probs * (nt(grad, values) - row_dot)).astype(bf16)
+            unstack(dq, base, part, head, nn(ds, keys) * scaling)
+            dk = tn(ds, query) * scaling
+            for ref, top in ((dkv, 0), (dkvp, 2 * part)):
+                for i in (0, 1):
+                    spot = pl.ds(base + i * 2 * part, part)
+                    low = top + i * part
+                    ref[spot, pl.ds(0, head)] = dk[low : low + part].astype(ref.dtype)
+                    ref[spot, pl.ds(head, head)] = dv[low : low + part].astype(ref.dtype)
+
+    kv_far = lines.start(dkvp, got, near[HIGH])
+
+    spill(4, z, wd, False)
+    sent = to_core()
+    spill(0, z, wd, False)
+    total, _ = sum_lines(near, lines, c, sent, from_core, kept, second_a, second_b, from_z, from_y, last_a, last_b, lambda: gate.pass_z(1))
+    for device in (CORE, LOW, ACROSS):
+        pl.semaphore_signal(done, inc=1, device_id=near[device], device_id_type=MESH)
+    own_out[...] = (h[...] + total).astype(bf16)
+    out_far = lines.start(own_out, out_hbm.at[at["y"]], near[ACROSS])
+    moves.save(own_out, out_hbm.at[at["y"]])
+    for dc in (0, 1):
+        outward.pass_z(dc)
+
+    kv_far.wait_recv()
+    gain_q = gains[2:3, 0:head]
+    gain_k = gains[3:4, 0:head]
+    small_q = jnp.zeros((1, head), f32)
+
+    def through(u, w, gain, cos, sin):
+        scale = root_scale(u)
+        n = u * scale
+        e = turn_back(w, cos, sin)
+        f = e * gain
+        grad = (scale * (f - n * jnp.mean(f * n, axis=-1, keepdims=True))).astype(bf16)
+        return grad, jnp.sum(e * n, axis=0, keepdims=True)
+
+    sums[2:4, 0:head] = jnp.zeros((2, head), f32)
+
+    @pl.loop(0, 8)
+    def _(n):
+        span = pl.ds(pl.multiple_of(n * part, part), part)
+        cos, sin = tables(extra, n)
+        for j in range(q_width // head):
+            cols = pl.ds(j * head, head)
+            dqkv[span, cols], add = through(raw[span, cols], dq[span, cols], gain_q, cos, sin)
+            sums[2:3, 0:head] += add
+        dk = dkv[span, pl.ds(0, head)] + got[span, pl.ds(0, head)].astype(f32)
+        dv = dkv[span, pl.ds(head, head)] + got[span, pl.ds(head, head)].astype(f32)
+        cols = pl.ds(q_width, head)
+        dqkv[span, cols], add = through(raw[span, cols], dk, gain_k, cos, sin)
+        sums[3:4, 0:head] += add
+        dqkv[span, pl.ds(q_width + head, head)] = dv.astype(bf16)
+
+    spill(4, dqkv, wqkv, True)
+    pl.semaphore_wait(done, 3)
+    sent = to_core()
+    get_a.wait()
+    eighths_of(inward, 1, lambda run: tn(columns(b, run), dqkv[...]))
+    for dzh, dc in ((1, 0), (1, 1), (0, 0), (0, 1)):
+        inward.send_x(dzh, dc)
+    spill(0, dqkv, wqkv, True)
+    eighths_of(inward, 0, lambda run: tn(columns(b, run), dqkv[...]))
+    get_x.wait()
+
+    def pump_in():
+        for dc in (0, 1):
+            inward.pass_z(dc)
+        for dc in (0, 1):
+            down.deliver(dc)
+
+    da, _ = sum_lines(near, lines, c, sent, from_core, kept, second_a, second_b, from_z, from_y, last_a, last_b, pump_in)
+    wide = x_mine[...].astype(f32)
+    r = root_scale(wide)
+    n_a = wide * r
+    sums[0:1, :] = jnp.sum(da * n_a, axis=0, keepdims=True)
+    f = da * gains[0:1, :]
+    own_in[...] = (dh[...] + r * (f - n_a * jnp.mean(f * n_a, axis=-1, keepdims=True))).astype(bf16)
+    in_far = lines.start(own_in, in_hbm.at[at["y"]], near[ACROSS])
+    moves.save(own_in, in_hbm.at[at["y"]])
+
+    ranks = small.shape[0]
+    for n in range(ranks):
+        small[n, 0:2, :] = sums[0:2, n * block : (n + 1) * block]
+        small[n, 2:4, :] = sums[2:4, 0:head]
+        small[n, 4:8, :] = jnp.zeros((4, block), f32)
+
+    def few(dx, dzh, dc):
+        return pl.ds((flip(at["x"], dx) * 2 + flip(at["c"], dc)) * ctx_count + flip(at["zh"], dzh) * 2, 2)
+
+    over_x = {k: lines.start(small.at[few(1, *k)], rx_s.at[2 * k[0] + k[1]], near[ACROSS_X]) for k in ((1, 0), (1, 1), (0, 0), (0, 1))}
+    over_z = []
+    for dc in (0, 1):
+        over_x[1, dc].wait_recv()
+        small[few(0, 1, dc)] += rx_s[2 + dc]
+        over_z.append(lines.start(small.at[few(0, 1, dc)], rz_s.at[dc], near[HIGH]))
+    for dc in (0, 1):
+        gate.deliver(dc)
+    for dc in (0, 1):
+        over_x[0, dc].wait_recv()
+        over_z[dc].wait_recv()
+        small[few(0, 0, dc)] += rx_s[dc] + rz_s[dc]
+    base = few(0, 0, 0).start
+    side = few(0, 0, 1).start
+    spread = [
+        lines.start(small.at[base + 1 - at["zl"]], ry_s.at[0], near[LOW]),
+        lines.start(small.at[side + at["zl"]], ry_s.at[1], near[CORE]),
+        lines.start(small.at[side + 1 - at["zl"]], ry_s.at[2], near[DIAG]),
+    ]
+    for dc in (0, 1):
+        outward.deliver(dc)
+    arrive(spread)
+    ry_s[3] = small[base + at["zl"]] + ry_s[0] + ry_s[1] + ry_s[2]
+    across = lines.start(ry_s.at[3], ry_s.at[4], near[ACROSS])
+    for dc in (0, 1):
+        inward.deliver(dc)
+    across.wait_recv()
+    small_out[...] = ry_s[3] + ry_s[4]
+    for unit in (down, gate, outward, inward):
+        unit.finish()
+    arrive((out_far, in_far))
+    lines.close()
+    moves.close()
+
+
+VM = pl.BlockSpec(memory_space=pltpu.VMEM)
+HB = pl.BlockSpec(memory_space=pl.ANY)
+
+
+def shaped(shape, dtype):
+    return jax.ShapeDtypeStruct(shape, dtype)
+
+
+def split_device(
+    block_input, doc_positions, out_cotangent, attn_gain, mlp_gain, query_gain, key_gain,
+    w_query, w_key, w_value, w_out, w_gate, w_up, w_down,
+):
+    dp_count = lax.axis_size(DP)
+    ctx_count = lax.axis_size(CTX)
+    rank_count = dp_count * ctx_count
+    at = place()
+    rank = at[DP] * ctx_count + at[CTX]
+    upper = at["y"] == 1
+    seqs, part, width = block_input.shape
+    block = attn_gain.shape[0]
+    head_piece = query_gain.shape[0]
+    head = head_piece * rank_count
+    own_p = jnp.where(upper, doc_positions[::-1], doc_positions).astype(f32)
+    inverse = rope_base ** (-2.0 * jnp.arange(head // 2).astype(f32) / head)
+    angles = own_p[:, :, None] * inverse
+    extra = jnp.stack(
+        [jnp.concatenate([jnp.cos(angles), jnp.sin(angles)], axis=2), jnp.broadcast_to(own_p[:, :, None], (seqs, part, head))],
+        axis=1,
+    )
+    small = jnp.stack([query_gain, key_gain]).astype(f32)
+    small = lax.dynamic_update_slice(jnp.zeros((2, head), f32), small, (0, rank * head_piece))
+    own_gains = jnp.concatenate([jnp.stack([attn_gain, mlp_gain]).astype(f32), small, jnp.zeros((4, block), f32)])
+
+    tokens = 4 * seqs * part
+    q_width = w_query.shape[1] // 4
+    hidden = w_gate.shape[1] // 4
+    bound = functools.partial
+    eighths = (8, part, width)
+    cut = width // 4
+    sum_room = [
+        pltpu.VMEM((4, part, width), bf16), pltpu.VMEM((3, part, width), bf16),
+        pltpu.VMEM((part, cut), bf16), pltpu.VMEM((part, width - cut), bf16),
+        pltpu.VMEM((2, part, cut), bf16), pltpu.VMEM((2, part, width - cut), bf16),
+        pltpu.VMEM((part, cut), bf16), pltpu.VMEM((part, width - cut), bf16),
+    ]
+    shapes = {
+        "a": ((tokens, width), bf16), "raw": ((tokens, q_width + head), f32), "q": ((tokens, q_width), bf16),
+        "kv": ((tokens, 2 * head), bf16), "kvp": ((tokens, 2 * head), bf16), "o": ((tokens, q_width), bf16),
+        "lse": ((tokens, q_width), f32), "h": ((part, width), f32), "b": (eighths, bf16), "z": ((tokens, hidden), bf16),
+        "gu": ((tokens, 2 * hidden), bf16), "c": (eighths, bf16), "extra": ((8, 2, part, head), f32), "gains": ((8, width), f32),
+        "wqkv": ((width, q_width + 2 * head), bf16), "wo": ((q_width, width), bf16),
+        "wgu": ((width, 2 * hidden), bf16), "wd": ((hidden, width), bf16),
+    }
+    room = {name: pltpu.VMEM(*spec) for name, spec in shapes.items()}
+    kept = pl.pallas_call(
+        bound(forward_kernel, ctx_count, block, head),
+        out_shape=[shaped(*spec) for spec in shapes.values()],
+        in_specs=[HB] * 11,
+        out_specs=[HB] * len(shapes),
+        scratch_shapes=[
+            pltpu.VMEM(eighths, bf16), room["extra"], pltpu.VMEM((rank_count, 8, block), f32),
+            room["wqkv"], room["wo"], room["wgu"], room["wd"], room["a"], room["raw"], room["q"], room["kv"], room["kvp"],
+            room["o"], room["lse"], *sum_room,
+            room["h"], room["b"], room["z"], room["gu"], room["c"], room["gains"],
+            pltpu.SemaphoreType.DMA((160,)), pltpu.SemaphoreType.DMA((160,)), pltpu.SemaphoreType.DMA((64,)),
+        ],
+        compiler_params=pltpu.CompilerParams(collective_id=0, has_side_effects=True, vmem_limit_bytes=63 * 1024 * 1024),
+    )(block_input, out_cotangent, extra, own_gains, w_query, w_key, w_value, w_out, w_gate, w_up, w_down)
+    kept = dict(zip(shapes, kept))
+    pair_shape = (seqs, part, width)
+    names = (
+        "a", "raw", "q", "kv", "kvp", "o", "lse", "h", "b", "z", "gu", "c", "extra", "gains", "wqkv", "wo", "wgu", "wd",
+    )
+    run = 2 * block
+    vmem = pltpu.VMEM
+    wide_q = q_width + 2 * head
+    outs = pl.pallas_call(
+        bound(backward_kernel, ctx_count, block, head),
+        out_shape=[
+            shaped(pair_shape, bf16), shaped(pair_shape, bf16),
+            shaped(w_query.shape, bf16), shaped(w_key.shape, bf16), shaped(w_value.shape, bf16), shaped(w_out.shape, bf16),
+            shaped(w_gate.shape, bf16), shaped(w_up.shape, bf16), shaped(w_down.shape, bf16), shaped((8, block), f32),
+        ],
+        in_specs=[HB] * (1 + len(names)),
+        out_specs=[HB] * 9 + [VM],
+        scratch_shapes=[
+            *(room[k] for k in ("c", "wd", "z", "gu", "wgu", "b", "q", "kv", "kvp", "o", "lse", "raw", "extra", "gains", "wqkv", "wo", "h")),
+            vmem((part, width), f32), vmem((part, width), bf16),
+            vmem((tokens, q_width), f32), vmem((tokens, 2 * head), f32), vmem((tokens, 2 * head), bf16), vmem((tokens, 2 * head), bf16),
+            vmem((tokens, q_width), bf16), vmem((tokens, wide_q), bf16),
+            vmem((hidden, width), bf16), vmem((q_width, width), bf16), vmem((width, wide_q), bf16),
+            vmem((4, hidden, run), bf16), vmem((2, hidden, run), bf16),
+            vmem((4, run, 2 * hidden), bf16), vmem((2, run, 2 * hidden), bf16),
+            vmem((4, q_width, run), bf16), vmem((2, q_width, run), bf16),
+            vmem((4, run, wide_q), bf16), vmem((2, run, wide_q), bf16),
+            *sum_room,
+            vmem((part, width), bf16), vmem((part, width), bf16), vmem((8, width), f32),
+            vmem((rank_count, 8, block), f32), vmem((4, 2, 8, block), f32), vmem((2, 2, 8, block), f32), vmem((5, 8, block), f32),
+            pltpu.SemaphoreType.DMA((160,)), pltpu.SemaphoreType.DMA((160,)), pltpu.SemaphoreType.DMA((64,)),
+            pltpu.SemaphoreType.REGULAR, pltpu.SemaphoreType.REGULAR,
+        ],
+        compiler_params=pltpu.CompilerParams(collective_id=1, has_side_effects=True, vmem_limit_bytes=67043328),
+    )(block_input, kept["a"].reshape(eighths), *(kept[k] for k in names[1:]))
+    small = outs[9]
+    slots = small[2:4].reshape(2, rank_count, head_piece)
+    slots = lax.dynamic_index_in_dim(slots, rank, 1, keepdims=False)
+    return (
+        outs[0], outs[1].astype(f32), small[0], small[1], slots[0], slots[1], *(grad.astype(f32) for grad in outs[2:9]),
+    )
 
 
 def rms_scale(value_rows):
@@ -53,17 +1022,17 @@
     float_type = jnp.float32
     half_type = jnp.bfloat16
     fetched = (
-        lax.all_gather(shards[0], ("dp", "ctx"), axis=0, tiled=True),
-        lax.all_gather(shards[1], ("dp", "ctx"), axis=0, tiled=True),
-        lax.all_gather(shards[2], ("dp", "ctx"), axis=0, tiled=True),
-        lax.all_gather(shards[3], ("dp", "ctx"), axis=0, tiled=True),
-        lax.all_gather(shards[4], ("dp", "ctx"), axis=0, tiled=True),
-        lax.all_gather(shards[5], ("dp", "ctx"), axis=0, tiled=True),
-        lax.all_gather(shards[6], ("dp", "ctx"), axis=0, tiled=True),
-        lax.all_gather(shards[7], ("dp", "ctx"), axis=1, tiled=True),
-        lax.all_gather(shards[8], ("dp", "ctx"), axis=0, tiled=True),
-        lax.all_gather(shards[9], ("dp", "ctx"), axis=0, tiled=True),
-        lax.all_gather(shards[10], ("dp", "ctx"), axis=1, tiled=True),
+        lax.all_gather(shards[0], (DP, CTX), axis=0, tiled=True),
+        lax.all_gather(shards[1], (DP, CTX), axis=0, tiled=True),
+        lax.all_gather(shards[2], (DP, CTX), axis=0, tiled=True),
+        lax.all_gather(shards[3], (DP, CTX), axis=0, tiled=True),
+        lax.all_gather(shards[4], (DP, CTX), axis=0, tiled=True),
+        lax.all_gather(shards[5], (DP, CTX), axis=0, tiled=True),
+        lax.all_gather(shards[6], (DP, CTX), axis=0, tiled=True),
+        lax.all_gather(shards[7], (DP, CTX), axis=1, tiled=True),
+        lax.all_gather(shards[8], (DP, CTX), axis=0, tiled=True),
+        lax.all_gather(shards[9], (DP, CTX), axis=0, tiled=True),
+        lax.all_gather(shards[10], (DP, CTX), axis=1, tiled=True),
     )
     gain_attn = fetched[0].astype(float_type)
     gain_mlp = fetched[1].astype(float_type)
@@ -75,8 +1044,8 @@
     kv_count = key_proj.shape[1] // head_size
     group_size = head_count // kv_count
     token_count = inputs_seq.shape[0]
-    ctx_count = lax.axis_size("ctx")
-    ctx_rank = lax.axis_index("ctx")
+    ctx_count = lax.axis_size(CTX)
+    ctx_rank = lax.axis_index(CTX)
     scaling = head_size ** (-0.5)
     query_index = ctx_rank * token_count + jnp.arange(token_count, dtype=jnp.int32)
     lowest = query_index - places
@@ -112,8 +1081,8 @@
         jnp.zeros((token_count, kv_count, group_size, head_size), float_type),
     )
     pieces = (
-        lax.all_gather(key_rot, "ctx", axis=0, tiled=True),
-        lax.all_gather(value_rows, "ctx", axis=0, tiled=True),
+        lax.all_gather(key_rot, CTX, axis=0, tiled=True),
+        lax.all_gather(value_rows, CTX, axis=0, tiled=True),
     )
     row_count = pieces[0].shape[0]
     key_piece = pieces[0].reshape(row_count, kv_count, head_size)
@@ -147,7 +1116,7 @@
     )
     log_total = peak + jnp.log(total)
     attn_out = lax.psum(
-        jnp.dot(attn_rows, out_proj, preferred_element_type=float_type).astype(jnp.bfloat16), "mp"
+        jnp.dot(attn_rows, out_proj, preferred_element_type=float_type).astype(jnp.bfloat16), MP
     ).astype(jnp.float32)
     middle = residual_in + attn_out
     scale_mlp = rms_scale(middle)
@@ -159,21 +1128,21 @@
     hidden_rows = (gate_rows * sigmoid_gate * up_rows).astype(half_type)
     mlp_out = lax.psum(
         jnp.dot(hidden_rows, down_proj, preferred_element_type=float_type).astype(jnp.bfloat16),
-        "mp",
+        MP,
     ).astype(jnp.float32)
     block_output = (middle + mlp_out).astype(half_type)
     refetched = (
-        lax.all_gather(shards[0], ("dp", "ctx"), axis=0, tiled=True),
-        lax.all_gather(shards[1], ("dp", "ctx"), axis=0, tiled=True),
-        lax.all_gather(shards[2], ("dp", "ctx"), axis=0, tiled=True),
-        lax.all_gather(shards[3], ("dp", "ctx"), axis=0, tiled=True),
-        lax.all_gather(shards[4], ("dp", "ctx"), axis=0, tiled=True),
-        lax.all_gather(shards[5], ("dp", "ctx"), axis=0, tiled=True),
-        lax.all_gather(shards[6], ("dp", "ctx"), axis=0, tiled=True),
-        lax.all_gather(shards[7], ("dp", "ctx"), axis=1, tiled=True),
-        lax.all_gather(shards[8], ("dp", "ctx"), axis=0, tiled=True),
-        lax.all_gather(shards[9], ("dp", "ctx"), axis=0, tiled=True),
-        lax.all_gather(shards[10], ("dp", "ctx"), axis=1, tiled=True),
+        lax.all_gather(shards[0], (DP, CTX), axis=0, tiled=True),
+        lax.all_gather(shards[1], (DP, CTX), axis=0, tiled=True),
+        lax.all_gather(shards[2], (DP, CTX), axis=0, tiled=True),
+        lax.all_gather(shards[3], (DP, CTX), axis=0, tiled=True),
+        lax.all_gather(shards[4], (DP, CTX), axis=0, tiled=True),
+        lax.all_gather(shards[5], (DP, CTX), axis=0, tiled=True),
+        lax.all_gather(shards[6], (DP, CTX), axis=0, tiled=True),
+        lax.all_gather(shards[7], (DP, CTX), axis=1, tiled=True),
+        lax.all_gather(shards[8], (DP, CTX), axis=0, tiled=True),
+        lax.all_gather(shards[9], (DP, CTX), axis=0, tiled=True),
+        lax.all_gather(shards[10], (DP, CTX), axis=1, tiled=True),
     )
     gain_attn = refetched[0].astype(float_type)
     gain_mlp = refetched[1].astype(float_type)
@@ -189,7 +1158,7 @@
     gate_proj_grad = dot_tn(mlp_input, gate_grad)
     up_proj_grad = dot_tn(mlp_input, up_grad)
     mlp_in_grad = lax.psum(
-        (dot_nt(gate_grad, gate_proj) + dot_nt(up_grad, up_proj)).astype(jnp.bfloat16), "mp"
+        (dot_nt(gate_grad, gate_proj) + dot_nt(up_grad, up_proj)).astype(jnp.bfloat16), MP
     ).astype(jnp.float32)
     mlp_gain_grad = jnp.sum(mlp_in_grad * normed_mlp, axis=0)
     normed_grad = mlp_in_grad * gain_mlp
@@ -205,8 +1174,8 @@
         "qkgd,qkgd->kgq", grad_group, attn_group, preferred_element_type=float_type
     )
     key_back, value_back = (
-        lax.all_gather(key_rot, "ctx", axis=0, tiled=True),
-        lax.all_gather(value_rows, "ctx", axis=0, tiled=True),
+        lax.all_gather(key_rot, CTX, axis=0, tiled=True),
+        lax.all_gather(value_rows, CTX, axis=0, tiled=True),
     )
 
     def back_block(query_sum, block_id):
@@ -274,7 +1243,7 @@
     )
     kv_grad = lax.psum_scatter(
         kv_terms.reshape(ctx_count * token_count, 2 * kv_count * head_size).astype(jnp.bfloat16),
-        "ctx",
+        CTX,
         scatter_dimension=0,
         tiled=True,
     ).astype(jnp.float32)
@@ -315,10 +1284,10 @@
                 + dot_nt(key_half, key_proj)
                 + dot_nt(value_half, value_proj)
             ).astype(jnp.bfloat16),
-            "mp",
+            MP,
         ).astype(jnp.float32),
-        lax.psum(query_gain_part.astype(jnp.bfloat16), "mp").astype(jnp.float32),
-        lax.psum(key_gain_part.astype(jnp.bfloat16), "mp").astype(jnp.float32),
+        lax.psum(query_gain_part.astype(jnp.bfloat16), MP).astype(jnp.float32),
+        lax.psum(key_gain_part.astype(jnp.bfloat16), MP).astype(jnp.float32),
     )
     attn_gain_grad = jnp.sum(attn_in_grad * normed_attn, axis=0)
     normed_in_grad = attn_in_grad * gain_attn
@@ -372,7 +1341,7 @@
         w_up,
         w_down,
     )
-    head_size = query_gain.shape[0] * lax.axis_size(("dp", "ctx"))
+    head_size = query_gain.shape[0] * lax.axis_size((DP, CTX))
     model_width = block_input.shape[2]
     query_width = w_query.shape[1]
     kv_width = w_key.shape[1]
@@ -399,17 +1368,17 @@
         output_list.append(output_rows)
         grad_list.append(input_rows)
     owned = (
-        lax.psum_scatter(totals[0], ("dp", "ctx"), scatter_dimension=0, tiled=True),
-        lax.psum_scatter(totals[1], ("dp", "ctx"), scatter_dimension=0, tiled=True),
-        lax.psum_scatter(totals[2], ("dp", "ctx"), scatter_dimension=0, tiled=True),
-        lax.psum_scatter(totals[3], ("dp", "ctx"), scatter_dimension=0, tiled=True),
-        lax.psum_scatter(totals[4], ("dp", "ctx"), scatter_dimension=0, tiled=True),
-        lax.psum_scatter(totals[5], ("dp", "ctx"), scatter_dimension=0, tiled=True),
-        lax.psum_scatter(totals[6], ("dp", "ctx"), scatter_dimension=0, tiled=True),
-        lax.psum_scatter(totals[7], ("dp", "ctx"), scatter_dimension=1, tiled=True),
-        lax.psum_scatter(totals[8], ("dp", "ctx"), scatter_dimension=0, tiled=True),
-        lax.psum_scatter(totals[9], ("dp", "ctx"), scatter_dimension=0, tiled=True),
-        lax.psum_scatter(totals[10], ("dp", "ctx"), scatter_dimension=1, tiled=True),
+        lax.psum_scatter(totals[0], (DP, CTX), scatter_dimension=0, tiled=True),
+        lax.psum_scatter(totals[1], (DP, CTX), scatter_dimension=0, tiled=True),
+        lax.psum_scatter(totals[2], (DP, CTX), scatter_dimension=0, tiled=True),
+        lax.psum_scatter(totals[3], (DP, CTX), scatter_dimension=0, tiled=True),
+        lax.psum_scatter(totals[4], (DP, CTX), scatter_dimension=0, tiled=True),
+        lax.psum_scatter(totals[5], (DP, CTX), scatter_dimension=0, tiled=True),
+        lax.psum_scatter(totals[6], (DP, CTX), scatter_dimension=0, tiled=True),
+        lax.psum_scatter(totals[7], (DP, CTX), scatter_dimension=1, tiled=True),
+        lax.psum_scatter(totals[8], (DP, CTX), scatter_dimension=0, tiled=True),
+        lax.psum_scatter(totals[9], (DP, CTX), scatter_dimension=0, tiled=True),
+        lax.psum_scatter(totals[10], (DP, CTX), scatter_dimension=1, tiled=True),
     )
     return (
         jnp.stack(output_list),
@@ -428,38 +1397,49 @@
     )
 
 
+def choose(mesh, arrays):
+    dp, ctx, mp = mesh.shape[DP], mesh.shape[CTX], mesh.shape[MP]
+    width = arrays[0].shape[2]
+    paired = dp == 4 and ctx == 4 and mp == 2
+    return split_device if paired and width % (dp * ctx * 128) == 0 else on_device
+
+
 def solution(mesh):
     in_specs = (
-        P("dp", "ctx", None),
-        P("dp", "ctx"),
-        P("dp", "ctx", None),
-        P(("dp", "ctx")),
-        P(("dp", "ctx")),
-        P(("dp", "ctx")),
-        P(("dp", "ctx")),
-        P(("dp", "ctx"), "mp"),
-        P(("dp", "ctx"), "mp"),
-        P(("dp", "ctx"), "mp"),
-        P("mp", ("dp", "ctx")),
-        P(("dp", "ctx"), "mp"),
-        P(("dp", "ctx"), "mp"),
-        P("mp", ("dp", "ctx")),
+        P(DP, CTX, None),
+        P(DP, CTX),
+        P(DP, CTX, None),
+        P((DP, CTX)),
+        P((DP, CTX)),
+        P((DP, CTX)),
+        P((DP, CTX)),
+        P((DP, CTX), MP),
+        P((DP, CTX), MP),
+        P((DP, CTX), MP),
+        P(MP, (DP, CTX)),
+        P((DP, CTX), MP),
+        P((DP, CTX), MP),
+        P(MP, (DP, CTX)),
     )
     out_specs = (
-        P("dp", "ctx", None),
-        P("dp", "ctx", None),
-        P(("dp", "ctx")),
-        P(("dp", "ctx")),
-        P(("dp", "ctx")),
-        P(("dp", "ctx")),
-        P(("dp", "ctx"), "mp"),
-        P(("dp", "ctx"), "mp"),
-        P(("dp", "ctx"), "mp"),
-        P("mp", ("dp", "ctx")),
-        P(("dp", "ctx"), "mp"),
-        P(("dp", "ctx"), "mp"),
-        P("mp", ("dp", "ctx")),
-    )
-    return jax.shard_map(
-        on_device, mesh=mesh, in_specs=in_specs, out_specs=out_specs, check_vma=False
-    )
+        P(DP, CTX, None),
+        P(DP, CTX, None),
+        P((DP, CTX)),
+        P((DP, CTX)),
+        P((DP, CTX)),
+        P((DP, CTX)),
+        P((DP, CTX), MP),
+        P((DP, CTX), MP),
+        P((DP, CTX), MP),
+        P(MP, (DP, CTX)),
+        P((DP, CTX), MP),
+        P((DP, CTX), MP),
+        P(MP, (DP, CTX)),
+    )
+
+    def run(*arrays):
+        return jax.shard_map(
+            choose(mesh, arrays), mesh=mesh, in_specs=in_specs, out_specs=out_specs, check_vma=False
+        )(*arrays)
+
+    return run

time: 1960 us -> 490 us (0.25)
  waiting for transfers between devices: 1340 us -> 0 us
  Pallas kernels: 0 us -> 472 us
  matrix products: 240 us -> 0 us
  blocking collectives: 240 us -> 0 us
  local copies, waits for them, and re-layouts: 61.3 us -> 3.15 us
  other arithmetic: 45.7 us -> 14 us
    reduce_scatter x9 -> x0, waiting for transfers between devices: 1020 us -> none  [the longest x1 248 us: on_device(): lax.psum_scatter(totals[8], ('dp', 'ctx'), scatter_dimension=0, tiled=True)]
    pallas_call x0 -> x2, Pallas kernels: none -> 472 us  [the longest x1 258 us: split_device(): pl.pallas_call(bound(backward_kernel, ctx_count, block, head), out_shape=...]
    all_gather x7 -> x0, waiting for transfers between devices: 288 us -> none  [the longest x1 100 us: micro_pass(): lax.all_gather(shards[8], ('dp', 'ctx'), axis=0, tiled=True)]
    dot_general x56 -> x0, matrix products: 240 us -> none  [the longest x14 106 us: dot_tn(): lax.dot_general(left, right, (((0,), (0,)), ((), ())), preferred_element_...]
    all_gather x6 -> x0, blocking collectives: 144 us -> none  [the longest x2 39.9 us: micro_pass(): lax.all_gather(value_rows, 'ctx', axis=0, tiled=True)]
    unnamed x2 -> x0, blocking collectives: 90.6 us -> none
    psum x3 -> x0, waiting for transfers between devices: 25.9 us -> none  [the longest x1 23.2 us: micro_pass(): lax.psum((dot_nt(gate_grad, gate_proj) + dot_nt(up_grad, up_proj)).astype...]
    unnamed x183 -> x19, local copies, waits for them, and re-layouts: 20.9 us -> 1.01 us
  transfers between devices with their start and end apart: 19 -> 0, of which waited for: 14 -> 0; matrix products, arithmetic and copies ran while one was open for 12% -> 0% of each run, Pallas kernels for 0% -> 0%
where the time goes in v1:
time: 490 us; the launch traced here: 489 us
  Pallas kernels  472 us (96%)
  other arithmetic  14 us (3%)
    pallas_call x1, Pallas kernels, split_device(): pl.pallas_call(bound(backward_kernel, ctx_count, block, head), out_shape=...  258 us
    pallas_call x1, Pallas kernels, split_device(): pl.pallas_call(bound(forward_kernel, ctx_count, block, head), out_shape=[...  214 us

profile of v1, /device:TPU:0, one launch (start us, length us, event | category | flops | bytes accessed | tf_op | source)
XLA Modules:
  0.0 489.5 jit_solution(11433742811529893767)
XLA Ops:
  0.7 0.7 maximum_convert_fusion.1
  1.3 0.1 dynamic_update_slice.3
  1.5 0.7 maximum_convert_fusion
  2.2 0.1 pad.2.clone
  2.3 0.7 maximum_maximum_fusion.gain_hbm
  2.9 0.7 rev.3
  3.6 0.7 select_convert_fusion
  4.3 0.5 multiply_cosine_fusion
  4.9 0.1 maximum_bitcast_fusion
  5.0 0.1 stack_broadcast_in_dim.2
  5.1 0.7 pad_maximum_fusion.extra_hbm
  5.8 213.5 %shard_map.237 = (bf16[1024,2048]{1,0:T(8,128)(2,1)}, f32[1024,384]{1,0:T(8,128)}, bf16[1024,256]{1,0:T(8,128)(2,1)}, bf16[1024,256]{1,0:T(8,128)(2,1)}, bf16[10...) custom-call(bf16[2,128,2048]{2,1,0:T(8,128)(2,1)} %x_hbm.3, ...), custom_call_target="tpu_custom_call" | custom-call | tf_op jit(solution)/shard_map/pallas_call | solution.py:922
  219.3 258.1 %shard_map.238 = (bf16[2,128,2048]{2,1,0:T(8,128)(2,1)}, bf16[2,128,2048]{2,1,0:T(8,128)(2,1)}, bf16[128,1024]{1,0:T(8,128)(2,1)}, bf16[128,512]{1,0:T(8,128)(2,...) custom-call(bf16[2,128,2048]{2,1,0:T(8,128)(2,1)} %x_hbm.3, ...), custom_call_target="tpu_custom_call" | custom-call | tf_op jit(solution)/shard_map/pallas_call | solution.py:944
  477.4 0.0 copy-start.3
  477.4 0.0 copy-start.2
  477.4 2.9 convert_element_type.44
  480.3 0.0 copy-done.3
  480.3 0.0 copy-start.1
  480.3 1.3 convert_element_type.49
  481.6 0.0 copy-done.2
  481.6 0.0 copy-start.5
  481.6 1.3 convert_element_type.50
  482.9 0.0 copy-start.4
  482.9 0.0 copy-start.7
  482.9 0.0 copy-done.1
  482.9 0.0 copy-start.6
  482.9 0.0 copy-start.8
  483.0 0.0 copy-start
  483.0 1.2 convert_element_type.51
  484.2 0.0 copy-done.5
  484.2 0.8 convert_element_type.45
  485.1 0.0 copy-done.4
  485.1 0.8 convert_element_type.48
  485.9 0.0 copy-done.7
  485.9 0.7 convert_element_type.46
  486.6 0.0 copy-done.6
  486.6 0.7 convert_element_type.47
  487.4 0.0 copy-done.8
  487.4 0.1 reshape.44
  487.4 0.5 dynamic-slice_bitcast_fusion
  488.0 0.5 slice_bitcast_fusion
  488.5 0.0 copy-done
  488.5 1.0 copy.29
  (4 shorter events, 0.0 us)
Async XLA Ops:
  477.4 2.9 copy-start.3
  477.4 4.2 copy-start.2
  480.3 2.6 copy-start.1
  481.6 2.6 copy-start.5
  482.9 2.1 copy-start.4
  482.9 3.0 copy-start.7
  482.9 3.7 copy-start.6
  482.9 4.4 copy-start.8
  483.0 5.5 %copy-start = (bf16[2,128,2048]{2,1,0:T(8,128)(2,1)S(1)}, bf16[2,128,2048]{2,1,0:T(8,128)(2,1)}, u32[]{:S(2)}) copy-start(bf16[2,128,2048]{2,1,0:T(8,128)(2,1)} %get-tuple-element.88) | copy-start | bytes 3145732

commit v2 on v1

--- a/solution.py
+++ b/solution.py
@@ -261,9 +261,9 @@
     ctx_count, block, head,
     x_hbm, c_hbm, extra_hbm, gain_hbm, wq, wk, wv, wo, wg, wu, wd,
     a_out, raw_out, q_out, kv_out, kvp_out, o_out, lse_out, h_out, b_out, z_out, gu_out, c_out, extra_out, gains_out,
-    wqkv_out, wo_out, wgu_out, wd_out,
+    wqkv_out, wo_out, wgu_out, wd_out, work_d_out,
     x, extra, gain_all, wqkv, w_o, wgu, w_d, a, raw, q, kv, kvp, o, lse, from_core, kept, second_a, second_b, from_z, from_y, last_a, last_b,
-    h, b_all, z, gu, c, gains, send, recv, local,
+    h, b_all, z, gu, c, gains, work_d, send, recv, local,
 ):
     at = place()
     near = neighbours(at)
@@ -276,16 +276,21 @@
     meet_all(near, (CORE, LOW, ACROSS, DIAG, HIGH, ACROSS_X))
 
     seq = [flip(at["y"], ds) for ds in (0, 1)]
-    x_low = lines.start(x_hbm.at[seq[0]], x.at[2], near[LOW])
-    e_low = lines.start(extra_hbm.at[0], extra.at[2], near[LOW])
     units = (
         Weight(env, wq, wqkv, True, 0, q_width),
         Weight(env, wk, wqkv, True, q_width, head),
         Weight(env, wv, wqkv, True, q_width + head, head),
     )
     scale = Gains(env, gain_hbm, gain_all, True, 0, 0)
-    for unit in (scale, *units):
+    w_out = Weight(env, wo, w_o, False, 0, q_width)
+    w_gate = Weight(env, wg, wgu, True, 0, hidden)
+    w_up = Weight(env, wu, wgu, True, hidden, hidden)
+    w_down = Weight(env, wd, w_d, False, 0, hidden)
+    for unit in (scale, *units, w_out):
         unit.exchange()
+    x_low = lines.start(x_hbm.at[seq[0]], x.at[2], near[LOW])
+    e_low = lines.start(extra_hbm.at[0], extra.at[2], near[LOW])
+    w_gate.exchange()
     x_core = [lines.start(x_hbm.at[seq[ds]], x.at[4 + ds], near[CORE]) for ds in (0, 1)]
     e_core = lines.start(extra_hbm, extra.at[pl.ds(4, 2)], near[CORE])
     x_own = [moves.start(x_hbm.at[seq[ds]], x.at[ds]) for ds in (0, 1)]
@@ -298,12 +303,10 @@
         scale.send_x(dc)
         in_qkv.send_z(dc)
         in_qkv.send_x(dc)
-    w_out = Weight(env, wo, w_o, False, 0, q_width)
-    w_gate = Weight(env, wg, wgu, True, 0, hidden)
-    w_up = Weight(env, wu, wgu, True, hidden, hidden)
-    w_down = Weight(env, wd, w_d, False, 0, hidden)
-    w_out.exchange()
-    w_gate.exchange()
+    w_out.ready()
+    for dc in (0, 1):
+        w_out.send_z(dc)
+        w_out.send_x(dc)
     x_far, x_across = share(near, lines, x, x_low)
     e_far, e_across = share(near, lines, extra, e_low)
     w_up.exchange()
@@ -313,10 +316,6 @@
     for dc in (0, 1):
         scale.pass_x(dc)
         in_qkv.pass_x(dc)
-    w_out.ready()
-    for dc in (0, 1):
-        w_out.send_z(dc)
-        w_out.send_x(dc)
     w_gate.ready()
     w_gate.send_z(0)
     scale.complete()
@@ -377,7 +376,6 @@
     c_low = lines.start(c_hbm.at[seq[0]], c.at[2], near[LOW])
     w_up.ready()
     for dc in (0, 1):
-        w_up.send_z(dc)
         w_up.send_x(dc)
     moves.save(kvp, kvp_out)
     scaling = head ** (-0.5)
@@ -419,21 +417,23 @@
     project(0)
 
     def pump_gate():
+        w_up.send_z(1)
         for dc in (0, 1):
             w_gate.pass_x(dc)
         w_down.ready()
         for dc in (0, 1):
-            w_down.send_z(dc)
             w_down.send_x(dc)
         return share(near, lines, c, c_low)
 
-    sums, (c_far, c_across) = sum_lines(near, lines, out, sent, from_core, kept, second_a, second_b, from_z, from_y, last_a, last_b, pump_gate)
+    sums, (c_far, c_across) = sum_lines(near, lines, out, sent, (from_core, kept, second_a, second_b, from_z, from_y, last_a, last_b), lambda: w_up.send_z(0), pump_gate)
     h[...] = h[...] + sums
     moves.save(h, h_out)
     wide = h[...]
     b_all[0] = (wide * root_scale(wide) * gains[1:2, :]).astype(bf16)
 
     def pump_up():
+        for dc in (0, 1):
+            w_down.send_z(dc)
         for dc in (0, 1):
             w_up.pass_x(dc)
         c_far.append(pass_on(near, lines, c, c_across))
@@ -461,8 +461,12 @@
     finish(c_own)
     arrive(c_core + c_far)
     moves.save(c, c_out)
-    for dc in (0, 1):
-        w_down.pass_x(dc)
+    down = Grad(env, work_d, False, None, None, ())
+    w_down.pass_x(0)
+    eighths_of(down, 1, lambda run: tn(z[...], columns(c, run)))
+    w_down.pass_x(1)
+    eighths_of(down, 0, lambda run: tn(z[...], columns(c, run)))
+    moves.save(work_d, work_d_out)
     w_down.complete()
     moves.save(w_d, wd_out)
     lines.close()
@@ -484,34 +488,53 @@
     return jnp.concatenate([ref[2 * m], ref[2 * m + 1]], axis=0)
 
 
-def sum_lines(near, lines, part, first, from_core, kept, second_a, second_b, from_z, from_y, last_a, last_b, pump):
-    width, cut = part.shape[2], from_z.shape[2]
-    a, b = pl.ds(0, cut), pl.ds(cut, width - cut)
-
-    def total(k):
-        first[k].wait_recv()
-        return part[k].astype(f32) + from_core[k].astype(f32)
-
-    kept[2] = total(3).astype(bf16)
-    y1 = lines.start(kept.at[2, :, b], from_y.at[1], near[ACROSS])
-    z1 = lines.start(kept.at[2, :, a], from_z.at[1], near[LOW])
-    kept[0] = total(1).astype(bf16)
-    y0 = lines.start(kept.at[0, :, b], from_y.at[0], near[ACROSS])
-    kept[1] = total(2).astype(bf16)
-    z0 = lines.start(kept.at[1, :, a], from_z.at[0], near[LOW])
-    y1.wait_recv()
-    second_b[...] = (kept[1, :, b].astype(f32) + from_y[1].astype(f32)).astype(bf16)
-    z2 = lines.start(second_b, last_b, near[LOW])
-    z1.wait_recv()
-    second_a[...] = (kept[0, :, a].astype(f32) + from_z[1].astype(f32)).astype(bf16)
-    y2 = lines.start(second_a, last_a, near[ACROSS])
+class Sum:
+    def __init__(self, near, lines, part, first, rooms):
+        self.near, self.lines, self.part, self.first = near, lines, part, first
+        self.from_core, self.kept, self.second_a, self.second_b, self.from_z, self.from_y, self.last_a, self.last_b = rooms
+        width, self.cut = part.shape[2], self.from_z.shape[2]
+        self.a, self.b = pl.ds(0, self.cut), pl.ds(self.cut, width - self.cut)
+
+    def total(self, k):
+        self.first[k].wait_recv()
+        return self.part[k].astype(f32) + self.from_core[k].astype(f32)
+
+    def begin(self):
+        lines, near, kept = self.lines, self.near, self.kept
+        kept[2] = self.total(3).astype(bf16)
+        self.y1 = lines.start(kept.at[2, :, self.b], self.from_y.at[1], near[ACROSS])
+        self.z1 = lines.start(kept.at[2, :, self.a], self.from_z.at[1], near[LOW])
+        kept[0] = self.total(1).astype(bf16)
+        self.y0 = lines.start(kept.at[0, :, self.b], self.from_y.at[0], near[ACROSS])
+        kept[1] = self.total(2).astype(bf16)
+        self.z0 = lines.start(kept.at[1, :, self.a], self.from_z.at[0], near[LOW])
+
+    def middle(self):
+        lines, near, kept = self.lines, self.near, self.kept
+        self.y1.wait_recv()
+        self.second_b[...] = (kept[1, :, self.b].astype(f32) + self.from_y[1].astype(f32)).astype(bf16)
+        self.z2 = lines.start(self.second_b, self.last_b, near[LOW])
+        self.z1.wait_recv()
+        self.second_a[...] = (kept[0, :, self.a].astype(f32) + self.from_z[1].astype(f32)).astype(bf16)
+        self.y2 = lines.start(self.second_a, self.last_a, near[ACROSS])
+
+    def end(self):
+        arrive((self.z0, self.y0, self.y2, self.z2))
+        self.lines.settle([self.z1, self.y1, self.y0, self.z0, self.y2, self.z2])
+        left = self.from_z[0].astype(f32) + self.last_a[...].astype(f32)
+        right = self.from_y[0].astype(f32) + self.last_b[...].astype(f32)
+        return jnp.concatenate([left, right], axis=1)
+
+
+def sum_lines(near, lines, part, first, rooms, early, pump):
+    parts = Sum(near, lines, part, first, rooms)
+    parts.begin()
+    early()
+    parts.middle()
     extra = pump()
-    mine = total(0)
-    arrive((z0, y0, y2, z2))
-    lines.settle([*first.values(), z1, y1, y0, z0, y2, z2])
-    left = mine[:, :cut] + from_z[0].astype(f32) + last_a[...].astype(f32)
-    right = mine[:, cut:] + from_y[0].astype(f32) + last_b[...].astype(f32)
-    return jnp.concatenate([left, right], axis=1), extra
+    mine = parts.total(0)
+    lines.settle(list(first.values()))
+    return mine + parts.end(), extra
 
 
 def spread_lines(near, lines, out, cut, pump):
@@ -539,14 +562,14 @@
 
 
 class Grad:
-    def __init__(self, env, work, by_rows, over_x, over_z, outs):
-        self.env, self.work, self.by_rows, self.outs = env, work, by_rows, outs
+    def __init__(self, env, work, by_rows, over_x, over_z, outs, span=slice(None)):
+        self.env, self.work, self.by_rows, self.outs, self.span = env, work, by_rows, outs, span
         self.from_x, self.from_z = over_x, over_z
         self.x, self.z, self.last, self.local = {}, {}, [], []
 
     def index(self, dx, dzh, dc):
         spot = pl.ds(run_start(self.env.at, dx, dzh, dc, self.env.ctx_count, self.env.block), 2 * self.env.block)
-        return (spot, slice(None)) if self.by_rows else (slice(None), spot)
+        return (spot, self.span) if self.by_rows else (self.span, spot)
 
     def send_x(self, dzh, dc):
         self.x[dzh, dc] = self.env.lines.start(
@@ -612,12 +635,12 @@
 def backward_kernel(
     ctx_count, block, head,
     x_hbm, a_hbm, raw_hbm, q_hbm, kv_hbm, kvp_hbm, o_hbm, lse_hbm, h_hbm, b_hbm, z_hbm, gu_hbm, c_hbm, extra_hbm, gains_hbm,
-    wqkv_hbm, wo_hbm, wgu_hbm, wd_hbm,
+    wqkv_hbm, wo_hbm, wgu_hbm, wd_hbm, work_hbm,
     out_hbm, in_hbm, g_query, g_key, g_value, g_out, g_gate, g_up, g_down, small_out,
     c, wd, z, gu, wgu, b, q, kv, kvp, o, lse, raw, extra, gains, wqkv, wo, h, dh, x_mine, dq, dkv, dkvp, got, do, dqkv,
-    work_d, work_o, work_q, rx_d, rz_d, rx_g, rz_g, rx_o, rz_o, rx_q, rz_q,
+    work_d, work_o, work_q, rx_d, rz_d, rx_g, rz_g, rx_u, rz_u, rx_o, rz_o, rx_q, rz_q,
     from_core, kept, second_a, second_b, from_z, from_y, last_a, last_b, own_out, own_in, sums, small, rx_s, rz_s, ry_s,
-    send, recv, local, ready, done,
+    send, recv, local, ready, done, free,
 ):
     at = place()
     near = neighbours(at)
@@ -629,8 +652,9 @@
     rows = 2 * part
     scaling = head ** (-0.5)
     fetch = moves.start
-    get_z, get_c, get_d, get_gu = fetch(z_hbm, z), fetch(c_hbm, c), fetch(wd_hbm, wd), fetch(gu_hbm, gu)
-    get_w, get_b = fetch(wgu_hbm, wgu), fetch(b_hbm, b)
+    get_work = fetch(work_hbm, work_d)
+    get_c, get_d, get_gu = fetch(c_hbm, c), fetch(wd_hbm, wd), fetch(gu_hbm, gu)
+    get_w, get_b, get_z = fetch(wgu_hbm, wgu), fetch(b_hbm, b), fetch(z_hbm, z)
     get_more = [fetch(*p) for p in ((h_hbm, h), (gains_hbm, gains), (wo_hbm, wo), (o_hbm, o))]
     get_rest = [
         fetch(*p)
@@ -639,16 +663,15 @@
     get_x = fetch(x_hbm.at[at["y"]], x_mine)
     meet_all(near, (CORE, LOW, ACROSS, DIAG, HIGH, ACROSS_X))
     down = Grad(env, work_d, False, rx_d, rz_d, ((g_down, 0, hidden),))
-    gate = Grad(env, wgu, True, rx_g, rz_g, ((g_gate, 0, hidden), (g_up, hidden, hidden)))
+    gate = Grad(env, wgu, True, rx_g, rz_g, ((g_gate, 0, hidden),), pl.ds(0, hidden))
+    up = Grad(env, wgu, True, rx_u, rz_u, ((g_up, hidden, hidden),), pl.ds(hidden, hidden))
     outward = Grad(env, work_o, False, rx_o, rz_o, ((g_out, 0, q_width),))
     inward = Grad(env, work_q, True, rx_q, rz_q, ((g_query, 0, q_width), (g_key, q_width, head), (g_value, q_width + head, head)))
 
-    get_z.wait()
-    get_c.wait()
-    eighths_of(down, 1, lambda run: tn(z[...], columns(c, run)))
+    get_work.wait()
     for dc in (0, 1):
         down.send_x(1, dc)
-    eighths_of(down, 0, lambda run: tn(z[...], columns(c, run)))
+    get_c.wait()
     get_d.wait()
     get_gu.wait()
     dh[...] = c[0].astype(f32)
@@ -680,24 +703,30 @@
     spill(4, gu, wgu, True)
     sent = to_core()
     spill(0, gu, wgu, True)
-    for dc in (0, 1):
-        down.pass_z(dc)
     get_b.wait()
-    eighths_of(gate, 1, lambda run: tn(columns(b, run), gu[...]))
-    for dc in (0, 1):
-        gate.send_x(1, dc)
-    eighths_of(gate, 0, lambda run: tn(columns(b, run), gu[...]))
-    for device in (CORE, LOW, ACROSS):
-        pl.semaphore_signal(ready, inc=1, device_id=near[device], device_id_type=MESH)
+    both = Grad(env, wgu, True, None, None, ())
+    eighths_of(both, 1, lambda run: tn(columns(b, run), gu[...]))
+    for unit in (gate, up):
+        for dc in (0, 1):
+            unit.send_x(1, dc)
     finish(get_more)
-
-    def pump_down():
+    rooms = (from_core, kept, second_a, second_b, from_z, from_y, last_a, last_b)
+
+    def tell(flag):
+        for name in (CORE, LOW, ACROSS):
+            pl.semaphore_signal(flag, inc=1, device_id=near[name], device_id_type=MESH)
+
+    def pump_gate():
         for dc in (0, 1):
             down.send_x(0, dc)
-        for dc in (0, 1):
-            gate.send_x(0, dc)
-
-    db, _ = sum_lines(near, lines, c, sent, from_core, kept, second_a, second_b, from_z, from_y, last_a, last_b, pump_down)
+        for unit in (gate, up):
+            for dc in (0, 1):
+                unit.send_x(0, dc)
+        eighths_of(both, 0, lambda run: tn(columns(b, run), gu[...]))
+        tell(ready)
+        down.pass_z(1)
+
+    db, _ = sum_lines(near, lines, c, sent, rooms, lambda: down.pass_z(0), pump_gate)
     wide = h[...]
     r = root_scale(wide)
     n_m = wide * r
@@ -707,20 +736,18 @@
     dh[...] = middle
     pl.semaphore_wait(ready, 3)
     b[0] = middle.astype(bf16)
-    spread = spread_lines(near, lines, b, from_z.shape[2], lambda: None)
-    gate.pass_z(0)
+
+    def pump_spread():
+        gate.pass_z(0)
+        up.pass_z(0)
+
+    spread = spread_lines(near, lines, b, from_z.shape[2], pump_spread)
 
     @pl.loop(0, 4)
     def _(m):
         span = pl.ds(pl.multiple_of(m * rows, rows), rows)
         do[span, :] = nt(pair(b, m), wo[...]).astype(bf16)
 
-    eighths_of(outward, 1, lambda run: tn(o[...], columns(b, run)))
-    for dzh, dc in ((1, 0), (1, 1), (0, 0), (0, 1)):
-        outward.send_x(dzh, dc)
-    eighths_of(outward, 0, lambda run: tn(o[...], columns(b, run)))
-    lines.settle(spread)
-    get_a = fetch(a_hbm, b)
     finish(get_rest)
 
     @pl.loop(0, 2)
@@ -751,23 +778,29 @@
                     ref[spot, pl.ds(head, head)] = dv[low : low + part].astype(ref.dtype)
 
     kv_far = lines.start(dkvp, got, near[HIGH])
+    get_z.wait()
+    gate.pass_z(1)
+    eighths_of(outward, 1, lambda run: tn(o[...], columns(b, run)))
+    for dzh, dc in ((1, 0), (1, 1), (0, 0), (0, 1)):
+        outward.send_x(dzh, dc)
+    eighths_of(outward, 0, lambda run: tn(o[...], columns(b, run)))
+    lines.settle(spread)
+    get_a = fetch(a_hbm, b)
 
     spill(4, z, wd, False)
     sent = to_core()
     spill(0, z, wd, False)
-    total, _ = sum_lines(near, lines, c, sent, from_core, kept, second_a, second_b, from_z, from_y, last_a, last_b, lambda: gate.pass_z(1))
-    for device in (CORE, LOW, ACROSS):
-        pl.semaphore_signal(done, inc=1, device_id=near[device], device_id_type=MESH)
-    own_out[...] = (h[...] + total).astype(bf16)
-    out_far = lines.start(own_out, out_hbm.at[at["y"]], near[ACROSS])
-    moves.save(own_out, out_hbm.at[at["y"]])
-    for dc in (0, 1):
-        outward.pass_z(dc)
+    outer = Sum(near, lines, c, sent, rooms)
+    outer.begin()
+    up.pass_z(1)
+    h[...] = h[...] + outer.total(0)
+    lines.settle(list(sent.values()))
+    tell(done)
+    outer.middle()
 
     kv_far.wait_recv()
     gain_q = gains[2:3, 0:head]
     gain_k = gains[3:4, 0:head]
-    small_q = jnp.zeros((1, head), f32)
 
     def through(u, w, gain, cos, sin):
         scale = root_scale(u)
@@ -802,16 +835,23 @@
     for dzh, dc in ((1, 0), (1, 1), (0, 0), (0, 1)):
         inward.send_x(dzh, dc)
     spill(0, dqkv, wqkv, True)
-    eighths_of(inward, 0, lambda run: tn(columns(b, run), dqkv[...]))
+    own_out[...] = (h[...] + outer.end()).astype(bf16)
+    tell(free)
+    out_far = lines.start(own_out, out_hbm.at[at["y"]], near[ACROSS])
+    moves.save(own_out, out_hbm.at[at["y"]])
+    for dc in (0, 1):
+        outward.pass_z(dc)
     get_x.wait()
 
     def pump_in():
+        eighths_of(inward, 0, lambda run: tn(columns(b, run), dqkv[...]))
         for dc in (0, 1):
             inward.pass_z(dc)
         for dc in (0, 1):
             down.deliver(dc)
 
-    da, _ = sum_lines(near, lines, c, sent, from_core, kept, second_a, second_b, from_z, from_y, last_a, last_b, pump_in)
+    pl.semaphore_wait(free, 3)
+    da, _ = sum_lines(near, lines, c, sent, rooms, lambda: None, pump_in)
     wide = x_mine[...].astype(f32)
     r = root_scale(wide)
     n_a = wide * r
@@ -836,8 +876,9 @@
         over_x[1, dc].wait_recv()
         small[few(0, 1, dc)] += rx_s[2 + dc]
         over_z.append(lines.start(small.at[few(0, 1, dc)], rz_s.at[dc], near[HIGH]))
-    for dc in (0, 1):
-        gate.deliver(dc)
+    for unit in (gate, up):
+        for dc in (0, 1):
+            unit.deliver(dc)
     for dc in (0, 1):
         over_x[0, dc].wait_recv()
         over_z[dc].wait_recv()
@@ -858,10 +899,28 @@
         inward.deliver(dc)
     across.wait_recv()
     small_out[...] = ry_s[3] + ry_s[4]
-    for unit in (down, gate, outward, inward):
+    for unit in (down, gate, up, outward, inward):
         unit.finish()
     arrive((out_far, in_far))
     lines.close()
+    moves.close()
+
+
+def widen_kernel(count, *refs):
+    source, target, narrow, wide = (refs[n * count : (n + 1) * count] for n in range(4))
+    moves = Moves(refs[4 * count])
+    begun = [moves.start(source[n], narrow[n]) for n in range(count)]
+    for n in range(count):
+        begun[n].wait()
+        steps = 8
+        rows = narrow[n].shape[0] // steps
+
+        @pl.loop(0, steps)
+        def _(m):
+            span = pl.ds(pl.multiple_of(m * rows, rows), rows)
+            wide[n][span, :] = narrow[n][span, :].astype(f32)
+
+        moves.save(wide[n], target[n])
     moves.close()
 
 
@@ -916,7 +975,7 @@
         "lse": ((tokens, q_width), f32), "h": ((part, width), f32), "b": (eighths, bf16), "z": ((tokens, hidden), bf16),
         "gu": ((tokens, 2 * hidden), bf16), "c": (eighths, bf16), "extra": ((8, 2, part, head), f32), "gains": ((8, width), f32),
         "wqkv": ((width, q_width + 2 * head), bf16), "wo": ((q_width, width), bf16),
-        "wgu": ((width, 2 * hidden), bf16), "wd": ((hidden, width), bf16),
+        "wgu": ((width, 2 * hidden), bf16), "wd": ((hidden, width), bf16), "work": ((hidden, width), bf16),
     }
     room = {name: pltpu.VMEM(*spec) for name, spec in shapes.items()}
     kept = pl.pallas_call(
@@ -928,7 +987,7 @@
             pltpu.VMEM(eighths, bf16), room["extra"], pltpu.VMEM((rank_count, 8, block), f32),
             room["wqkv"], room["wo"], room["wgu"], room["wd"], room["a"], room["raw"], room["q"], room["kv"], room["kvp"],
             room["o"], room["lse"], *sum_room,
-            room["h"], room["b"], room["z"], room["gu"], room["c"], room["gains"],
+            room["h"], room["b"], room["z"], room["gu"], room["c"], room["gains"], room["work"],
             pltpu.SemaphoreType.DMA((160,)), pltpu.SemaphoreType.DMA((160,)), pltpu.SemaphoreType.DMA((64,)),
         ],
         compiler_params=pltpu.CompilerParams(collective_id=0, has_side_effects=True, vmem_limit_bytes=63 * 1024 * 1024),
@@ -936,7 +995,7 @@
     kept = dict(zip(shapes, kept))
     pair_shape = (seqs, part, width)
     names = (
-        "a", "raw", "q", "kv", "kvp", "o", "lse", "h", "b", "z", "gu", "c", "extra", "gains", "wqkv", "wo", "wgu", "wd",
+        "a", "raw", "q", "kv", "kvp", "o", "lse", "h", "b", "z", "gu", "c", "extra", "gains", "wqkv", "wo", "wgu", "wd", "work",
     )
     run = 2 * block
     vmem = pltpu.VMEM
@@ -957,23 +1016,34 @@
             vmem((tokens, q_width), bf16), vmem((tokens, wide_q), bf16),
             vmem((hidden, width), bf16), vmem((q_width, width), bf16), vmem((width, wide_q), bf16),
             vmem((4, hidden, run), bf16), vmem((2, hidden, run), bf16),
-            vmem((4, run, 2 * hidden), bf16), vmem((2, run, 2 * hidden), bf16),
+            vmem((4, run, hidden), bf16), vmem((2, run, hidden), bf16),
+            vmem((4, run, hidden), bf16), vmem((2, run, hidden), bf16),
             vmem((4, q_width, run), bf16), vmem((2, q_width, run), bf16),
             vmem((4, run, wide_q), bf16), vmem((2, run, wide_q), bf16),
             *sum_room,
             vmem((part, width), bf16), vmem((part, width), bf16), vmem((8, width), f32),
             vmem((rank_count, 8, block), f32), vmem((4, 2, 8, block), f32), vmem((2, 2, 8, block), f32), vmem((5, 8, block), f32),
             pltpu.SemaphoreType.DMA((160,)), pltpu.SemaphoreType.DMA((160,)), pltpu.SemaphoreType.DMA((64,)),
-            pltpu.SemaphoreType.REGULAR, pltpu.SemaphoreType.REGULAR,
+            pltpu.SemaphoreType.REGULAR, pltpu.SemaphoreType.REGULAR, pltpu.SemaphoreType.REGULAR,
         ],
         compiler_params=pltpu.CompilerParams(collective_id=1, has_side_effects=True, vmem_limit_bytes=67043328),
     )(block_input, kept["a"].reshape(eighths), *(kept[k] for k in names[1:]))
     small = outs[9]
     slots = small[2:4].reshape(2, rank_count, head_piece)
     slots = lax.dynamic_index_in_dim(slots, rank, 1, keepdims=False)
-    return (
-        outs[0], outs[1].astype(f32), small[0], small[1], slots[0], slots[1], *(grad.astype(f32) for grad in outs[2:9]),
-    )
+    narrow = (outs[1].reshape(seqs * part, width), *outs[2:9])
+    wide = pl.pallas_call(
+        bound(widen_kernel, len(narrow)),
+        out_shape=[shaped(array.shape, f32) for array in narrow],
+        in_specs=[HB] * len(narrow),
+        out_specs=[HB] * len(narrow),
+        scratch_shapes=[
+            *(vmem(array.shape, bf16) for array in narrow), *(vmem(array.shape, f32) for array in narrow),
+            pltpu.SemaphoreType.DMA((2 * len(narrow),)),
+        ],
+        compiler_params=pltpu.CompilerParams(vmem_limit_bytes=48 * 1024 * 1024),
+    )(*narrow)
+    return (outs[0], wide[0].reshape(pair_shape), small[0], small[1], slots[0], slots[1], *wide[1:])
 
 
 def rms_scale(value_rows):

time: 490 us -> 468 us (0.955); the launches traced: 489 us -> 462 us
  Pallas kernels: 472 us -> 446 us
  other arithmetic: 14 us -> 4.08 us
  local copies, waits for them, and re-layouts: 3.15 us -> 11.4 us
    pallas_call x1, Pallas kernels: 258 us -> 226 us  [split_device(): pl.pallas_call(bound(backward_kernel, ctx_count, block, head), out_shape=...]
    convert_element_type x8 -> x0, other arithmetic: 9.87 us -> none  [the longest x7 6.97 us: split_device(): grad.astype(f32)]
    unnamed x19 -> x21, local copies, waits for them, and re-layouts: 1.01 us -> 9.3 us
where the time goes in v2:
time: 468 us; the launch traced here: 462 us
  Pallas kernels  446 us (95%)
  local copies, waits for them, and re-layouts  11.4 us (2%)
    pallas_call x1, Pallas kernels, split_device(): pl.pallas_call(bound(backward_kernel, ctx_count, block, head), out_shape=...  226 us
    pallas_call x1, Pallas kernels, split_device(): pl.pallas_call(bound(forward_kernel, ctx_count, block, head), out_shape=[...  216 us

profile of v2, /device:TPU:0, one launch (start us, length us, event | category | flops | bytes accessed | tf_op | source)
XLA Modules:
  0.0 462.3 jit_solution(10305778902742883403)
XLA Ops:
  0.7 0.7 maximum_convert_fusion.1
  1.3 0.1 dynamic_update_slice.3
  1.5 0.7 maximum_convert_fusion
  2.2 0.1 pad.2.clone
  2.3 0.7 maximum_maximum_fusion.gain_hbm
  2.9 0.7 rev.3
  3.6 0.7 select_convert_fusion
  4.3 0.5 multiply_cosine_fusion
  4.9 0.1 maximum_bitcast_fusion
  5.0 0.1 stack_broadcast_in_dim.2
  5.1 0.7 pad_maximum_fusion.extra_hbm
  5.8 215.8 %shard_map.237 = (bf16[1024,2048]{1,0:T(8,128)(2,1)}, f32[1024,384]{1,0:T(8,128)}, bf16[1024,256]{1,0:T(8,128)(2,1)}, bf16[1024,256]{1,0:T(8,128)(2,1)}, bf16[10...) custom-call(bf16[2,128,2048]{2,1,0:T(8,128)(2,1)} %x_hbm.3, ...), custom_call_target="tpu_custom_call" | custom-call | tf_op jit(solution)/shard_map/pallas_call | solution.py:981
  221.6 226.0 %shard_map.238 = (bf16[2,128,2048]{2,1,0:T(8,128)(2,1)}, bf16[2,128,2048]{2,1,0:T(8,128)(2,1)}, bf16[128,1024]{1,0:T(8,128)(2,1)}, bf16[128,512]{1,0:T(8,128)(2,...) custom-call(bf16[2,128,2048]{2,1,0:T(8,128)(2,1)} %x_hbm.3, ...), custom_call_target="tpu_custom_call" | custom-call | tf_op jit(solution)/shard_map/pallas_call | solution.py:1003
  447.6 0.0 copy-start.9
  447.6 0.0 copy-start
  447.6 1.2 copy-done
  448.8 0.0 copy-start.1
  448.8 1.1 copy-done.1
  450.0 0.0 copy-start.2
  450.0 1.1 copy-done.2
  451.1 0.0 copy-start.3
  451.1 1.1 copy-done.3
  452.2 0.0 copy-start.4
  452.2 0.9 copy-done.4
  453.2 0.0 copy-start.5
  453.2 0.9 copy-done.5
  454.1 0.0 copy-start.6
  454.1 0.9 copy-done.6
  455.0 0.0 copy-start.7
  455.0 0.9 copy-done.7
  455.9 0.0 copy-start.8
  455.9 4.2 shard_map.239
  460.2 0.0 copy-done.9
  460.2 0.1 reshape.52
  460.3 0.5 dynamic-slice_bitcast_fusion
  460.8 0.5 slice_bitcast_fusion
  461.3 0.0 copy-done.8
  461.3 1.0 copy.29
  (4 shorter events, 0.0 us)
Async XLA Ops:
  447.6 12.6 %copy-start.9 = (f32[8,128]{1,0:T(8,128)S(1)}, f32[8,128]{1,0:T(8,128)}, u32[]{:S(2)}) copy-start(f32[8,128]{1,0:T(8,128)} %get-tuple-element.79) | copy-start | bytes 12292
  447.6 1.2 copy-start
  448.8 1.1 copy-start.1
  450.0 1.1 copy-start.2
  451.1 1.1 copy-start.3
  452.2 0.9 copy-start.4
  453.2 0.9 copy-start.5
  454.1 0.9 copy-start.6
  455.0 0.9 copy-start.7
  455.9 5.4 %copy-start.8 = (bf16[2,128,2048]{2,1,0:T(8,128)(2,1)S(1)}, bf16[2,128,2048]{2,1,0:T(8,128)(2,1)}, u32[]{:S(2)}) copy-start(bf16[2,128,2048]{2,1,0:T(8,128)(2,1)} %get-tuple-element.106) | copy-start | bytes 3145732

commit v3 on v2

--- a/solution.py
+++ b/solution.py
@@ -445,6 +445,7 @@
 
     w_up.complete()
     moves.save(wgu, wgu_out)
+    w_down.pass_x(0)
 
     @pl.loop(0, 4)
     def _(m):
@@ -462,9 +463,8 @@
     arrive(c_core + c_far)
     moves.save(c, c_out)
     down = Grad(env, work_d, False, None, None, ())
-    w_down.pass_x(0)
+    w_down.pass_x(1)
     eighths_of(down, 1, lambda run: tn(z[...], columns(c, run)))
-    w_down.pass_x(1)
     eighths_of(down, 0, lambda run: tn(z[...], columns(c, run)))
     moves.save(work_d, work_d_out)
     w_down.complete()
@@ -724,9 +724,10 @@
                 unit.send_x(0, dc)
         eighths_of(both, 0, lambda run: tn(columns(b, run), gu[...]))
         tell(ready)
+        down.pass_z(0)
         down.pass_z(1)
 
-    db, _ = sum_lines(near, lines, c, sent, rooms, lambda: down.pass_z(0), pump_gate)
+    db, _ = sum_lines(near, lines, c, sent, rooms, lambda: None, pump_gate)
     wide = h[...]
     r = root_scale(wide)
     n_m = wide * r

time: 468 us -> 465 us (level)
  no operation moved by 1% of the time
where the time goes in v3:
time: 465 us; the launch traced here: 461 us
  Pallas kernels  445 us (96%)
  local copies, waits for them, and re-layouts  11.4 us (2%)
    pallas_call x1, Pallas kernels, split_device(): pl.pallas_call(bound(backward_kernel, ctx_count, block, head), out_shape=...  228 us
    pallas_call x1, Pallas kernels, split_device(): pl.pallas_call(bound(forward_kernel, ctx_count, block, head), out_shape=[...  213 us
    unnamed x21, local copies, waits for them, and re-layouts  9.3 us

profile of v3, /device:TPU:0, one launch (start us, length us, event | category | flops | bytes accessed | tf_op | source)
XLA Modules:
  0.0 461.4 jit_solution(9789584040803986668)
XLA Ops:
  0.7 0.7 maximum_convert_fusion.1
  1.3 0.1 dynamic_update_slice.3
  1.5 0.7 maximum_convert_fusion
  2.2 0.1 pad.2.clone
  2.3 0.7 maximum_maximum_fusion.gain_hbm
  2.9 0.7 rev.3
  3.6 0.7 select_convert_fusion
  4.3 0.5 multiply_cosine_fusion
  4.9 0.1 maximum_bitcast_fusion
  5.0 0.1 stack_broadcast_in_dim.2
  5.1 0.7 pad_maximum_fusion.extra_hbm
  5.8 213.3 %shard_map.237 = (bf16[1024,2048]{1,0:T(8,128)(2,1)}, f32[1024,384]{1,0:T(8,128)}, bf16[1024,256]{1,0:T(8,128)(2,1)}, bf16[1024,256]{1,0:T(8,128)(2,1)}, bf16[10...) custom-call(bf16[2,128,2048]{2,1,0:T(8,128)(2,1)} %x_hbm.3, ...), custom_call_target="tpu_custom_call" | custom-call | tf_op jit(solution)/shard_map/pallas_call | solution.py:982
  219.1 227.5 %shard_map.238 = (bf16[2,128,2048]{2,1,0:T(8,128)(2,1)}, bf16[2,128,2048]{2,1,0:T(8,128)(2,1)}, bf16[128,1024]{1,0:T(8,128)(2,1)}, bf16[128,512]{1,0:T(8,128)(2,...) custom-call(bf16[2,128,2048]{2,1,0:T(8,128)(2,1)} %x_hbm.3, ...), custom_call_target="tpu_custom_call" | custom-call | tf_op jit(solution)/shard_map/pallas_call | solution.py:1004
  446.7 0.0 copy-start.9
  446.7 0.0 copy-start
  446.7 1.2 copy-done
  447.9 0.0 copy-start.1
  447.9 1.1 copy-done.1
  449.1 0.0 copy-start.2
  449.1 1.1 copy-done.2
  450.2 0.0 copy-start.3
  450.2 1.1 copy-done.3
  451.3 0.0 copy-start.4
  451.3 0.9 copy-done.4
  452.3 0.0 copy-start.5
  452.3 0.9 copy-done.5
  453.2 0.0 copy-start.6
  453.2 0.9 copy-done.6
  454.1 0.0 copy-start.7
  454.1 0.9 copy-done.7
  455.0 0.0 copy-start.8
  455.0 4.2 shard_map.239
  459.3 0.0 copy-done.9
  459.3 0.1 reshape.52
  459.4 0.5 dynamic-slice_bitcast_fusion
  459.9 0.5 slice_bitcast_fusion
  460.4 0.0 copy-done.8
  460.4 1.0 copy.29
  (4 shorter events, 0.0 us)
Async XLA Ops:
  446.7 12.6 %copy-start.9 = (f32[8,128]{1,0:T(8,128)S(1)}, f32[8,128]{1,0:T(8,128)}, u32[]{:S(2)}) copy-start(f32[8,128]{1,0:T(8,128)} %get-tuple-element.79) | copy-start | bytes 12292
  446.7 1.2 copy-start
  447.9 1.1 copy-start.1
  449.1 1.1 copy-start.2
  450.2 1.1 copy-start.3
  451.3 0.9 copy-start.4
  452.3 0.9 copy-start.5
  453.2 0.9 copy-start.6
  454.1 0.9 copy-start.7
  455.0 5.4 %copy-start.8 = (bf16[2,128,2048]{2,1,0:T(8,128)(2,1)S(1)}, bf16[2,128,2048]{2,1,0:T(8,128)(2,1)}, u32[]{:S(2)}) copy-start(bf16[2,128,2048]{2,1,0:T(8,128)(2,1)} %get-tuple-element.106) | copy-start | bytes 3145732
